TPU v7x, 512 devices: a whole 4x4x16 slice. The times are simulated.
512 devices in a mesh: group: 8 (over x, y_hi), vocab: 64 (over z, y_lo, core).
Axes of the slice: x: 4, y: 4 (y_hi: 2, y_lo: 2; y = y_hi * 2 + y_lo), z: 16, core: 2. Of those that a mesh axis runs over, the one named last changes fastest.
Arguments:
- table: bfloat16 [4608, 196608], P('vocab', 'group')
- hidden: bfloat16 [448, 4608], P(None, 'vocab')
- gain: bfloat16 [4608], P('vocab'), may hold values from 0.099609375 to 1.8984375
- ids: int32 [448], replicated, may hold values from 0 to 196607
Outputs:
- next_embed: bfloat16 [448, 4608], P(None, 'vocab')
- logprobs: float32 [448, 196608], P(None, ('group', 'vocab'))
- chosen: float32 [448], replicated
All inputs are finite; a program needn't handle non-finite values.
Results may differ from a plain program's by a relative error of at most 0.001.
Values may be sent and summed in bfloat16 or wider, within the bound.
No kernel may reach another device: no remote copies, remote signals or barrier semaphores. Data moves between devices by JAX's collectives and lax.ppermute only.
A program may use at most 64 MiB of HBM per device.

v0:
```python
import math

import jax
import jax.numpy as jnp
from jax import lax
from jax.sharding import Mesh
from jax.sharding import PartitionSpec as P

VOCAB = ("vocab_0", "vocab_1", "vocab_2")
GROUP = ("group_0", "group_1")
GROUP_VOCAB = ("group_0", "group_1", "vocab_0", "vocab_1", "vocab_2")


def gather_turned(arrays, axis, dims):
    turned = [jnp.moveaxis(a, dim, 0) for a, dim in zip(arrays, dims)]
    both = jnp.concatenate([t.reshape(len(t), -1) for t in turned], axis=1)
    out, at, done = (lax.all_gather(both, axis, axis=0, tiled=True), 0, [])
    for t, dim in zip(turned, dims):
        slab = out[:, at : at + t[0].size].reshape(-1, *t.shape[1:])
        done.append(jnp.moveaxis(slab, 0, dim))
        at += t[0].size
    return tuple(done)


def in_blocks(array, dim, size):
    before, after = (array.shape[:dim], array.shape[dim + 1 :])
    return jnp.moveaxis(array.reshape(*before, size, -1, *after), dim, 0)


def cut_rows(length, count):
    lap = length // count
    if lap >= 8:
        lap -= lap % 8
    return [lap * k for k in range(1, count)]


def in_order(blocks, dim):
    lengths = list(blocks.shape[1:])
    lengths[dim] *= blocks.shape[0]
    return jnp.moveaxis(blocks, 0, dim).reshape(lengths)


def several_exchanges(array, axis, pieces, split_dim, concat_dim):
    blocks = in_blocks(array, split_dim, lax.axis_size(axis))
    widest = max(range(1, max(2, blocks.ndim - 1)), key=lambda d: blocks.shape[d])
    done = []
    for slab in jnp.split(blocks, cut_rows(blocks.shape[widest], pieces), axis=widest):
        if slab.size:
            done.append(lax.all_to_all(slab, axis, split_axis=0, concat_axis=0, tiled=True))
    return in_order(jnp.concatenate(done, axis=widest), concat_dim)


def over_axes(array, axes):
    for axis in axes:
        array = lax.psum(array, axis)
    return array


def body(table, hidden, gain, ids):
    share, span_cols = table.shape
    groups_n = lax.axis_size(VOCAB)
    voc_cols = span_cols // groups_n
    width = share * groups_n
    group_index = lax.axis_index(GROUP)
    vocab_index = lax.axis_index(VOCAB)
    local_ids = ids - group_index * span_cols
    inside = jnp.logical_and(local_ids >= 0, local_ids < span_cols)
    found = jnp.take(table, jnp.clip(local_ids, 0, span_cols - 1), axis=1).astype(jnp.float32).T
    found = found * inside[:, None].astype(jnp.float32)
    embed_cols = lax.psum(found.astype(jnp.bfloat16), GROUP).astype(jnp.float32)
    next_embed = (embed_cols * math.sqrt(width)).astype(jnp.bfloat16)
    whole, gain_all = gather_turned((hidden, gain), VOCAB, (1, 0))
    states = whole.astype(jnp.float32)
    mean_sq = jnp.sum(states * states, axis=1, keepdims=True) / width
    normed = (states * gain_all.astype(jnp.float32) * lax.rsqrt(mean_sq + 1e-06)).astype(
        jnp.bfloat16
    )
    full_cols = several_exchanges(table, VOCAB, 2, 1, 0)
    logits = jnp.dot(normed, full_cols, preferred_element_type=jnp.float32)
    capped = 30.0 * jnp.tanh(logits / 30.0)
    first_col = (group_index * groups_n + vocab_index) * voc_cols
    offsets = ids - first_col
    columns = lax.broadcasted_iota(jnp.int32, capped.shape, 1)
    pick = jnp.sum(jnp.where(columns == offsets[:, None], capped, 0.0), axis=1)
    sums, picks = (
        over_axes(jnp.sum(jnp.exp(capped), axis=1), GROUP_VOCAB),
        over_axes(pick, GROUP_VOCAB),
    )
    log_total = jnp.log(sums)
    logprobs = capped - log_total[:, None]
    chosen = picks - log_total
    return (next_embed, logprobs, chosen)


def solution(mesh):
    torus = Mesh(
        mesh.devices.reshape(4, 2, 16, 2, 2),
        ("group_0", "group_1", "vocab_0", "vocab_1", "vocab_2"),
    )
    return jax.shard_map(
        body,
        mesh=torus,
        in_specs=(P(VOCAB, GROUP), P(None, VOCAB), P(VOCAB), P()),
        out_specs=(P(None, VOCAB), P(None, GROUP_VOCAB), P()),
        check_vma=False,
    )
```

profile of v0, /device:TPU:1, one launch (start us, length us, event | category | flops | bytes accessed | tf_op | source)
XLA Modules:
  0.0 301.4 jit_solution(11320559064461386992)
XLA Ops:
  7.2 2.8 copy.22
  9.9 0.0 copy-start.3
  9.9 0.2 split.8
  10.1 2.1 copy.19
  12.2 18.3 %all-to-all-start = ((bf16[64,32,384]{2,1,0:T(8,128)(2,1)}), bf16[64,32,384]{2,1,0:T(8,128)(2,1)}, u32[]{:S(2)}, u32[]{:S(2)}) async-start(bf16[64,32,384]{2,1,0:T(8,128)(2,1)} %copy.19), calls=%async_computation | async-start | bytes 3145728 | tf_op jit(solution)/shard_map/all_to_all | solution.py:49
  30.5 0.0 all-gather.2.cloned.1.call-start
  30.5 0.0 copy-done.3
  30.6 0.7 copy.18
  31.3 1.6 pad_maximum_fusion.1
  32.9 0.0 all-gather.2.cloned.1.call-update
  32.9 0.2 split.9
  33.1 0.0 copy-start
  33.1 2.4 copy.20
  35.6 79.7 %all-to-all-done = bf16[64,32,384]{2,1,0:T(8,128)(2,1)} async-done(((bf16[64,32,384]{2,1,0:T(8,128)(2,1)}), bf16[64,32,384]{2,1,0:T(8,128)(2,1)}, u32[]{:S(2)}, u32[]{:S(2)}) %all-to-all-start) | async-done | bytes 1572896 | tf_op jit(solution)/shard_map/all_to_all | solution.py:49
  115.3 6.8 %all-to-all-start.1 = ((bf16[64,40,384]{2,1,0:T(8,128)(2,1)}), bf16[64,40,384]{2,1,0:T(8,128)(2,1)}, u32[]{:S(2)}, u32[]{:S(2)}) async-start(bf16[64,40,384]{2,1,0:T(8,128)(2,1)} %copy.20), calls=%async_computation.1 | async-start | bytes 3932160 | tf_op jit(solution)/shard_map/all_to_all | solution.py:49
  122.1 0.0 copy-done
  122.1 0.0 copy-start.2
  122.1 5.3 %copy.17 = bf16[72,24576]{0,1:T(8,128)(2,1)} copy(bf16[72,24576]{1,0:T(8,128)(2,1)S(1)} %copy-done) | data formatting | bytes 7077888 | tf_op args[0]
  127.4 0.0 copy-done.2
  127.4 4.8 %gather_fusion = bf16[448,72]{1,0:T(8,128)(2,1)S(1)} fusion(bf16[72,24576]{0,1:T(8,128)(2,1)} %copy.17, s32[1024]{0:T(1024)S(1)} %pad_clamp_fusion), kind=kCustom, calls=%fused_computation | custom fusion | bytes 130816 | tf_op jit(solution)/shard_map/jit(_take)/gather | solution.py:68
  132.2 0.2 multiply_convert_fusion
  132.4 38.7 %psum.77 = bf16[448,72]{1,0:T(8,128)(2,1)S(1)} all-reduce(bf16[448,72]{1,0:T(8,128)(2,1)S(1)} %multiply_convert_fusion), channel_id=1, replica_groups=mesh['group_0'=4,'group_1'=2,'vocab_0'=16,'vocab_1'=2,'vocab_2'=2] {'gro..., use_global_device_ids=true, to_apply=%region_0.1 | all-reduce | flops 32256 | bytes 129024 | tf_op jit(solution)/shard_map/psum | solution.py:70
  171.1 0.7 copy.21
  171.9 55.3 %all-to-all-done.1 = bf16[64,40,384]{2,1,0:T(8,128)(2,1)} async-done(((bf16[64,40,384]{2,1,0:T(8,128)(2,1)}), bf16[64,40,384]{2,1,0:T(8,128)(2,1)}, u32[]{:S(2)}, u32[]{:S(2)}) %all-to-all-start.1) | async-done | bytes 1966112 | tf_op jit(solution)/shard_map/all_to_all | solution.py:49
  227.1 2.4 pad_maximum_fusion
  229.5 0.0 all-gather.2.cloned.1.call-done
  229.5 0.0 copy-start.1
  229.5 3.6 %fusion.2 = f32[448]{0:T(512)S(1)} fusion(bf16[4608,449]{1,0:T(8,128)(2,1)} %all-gather.2.cloned.1.call-done), kind=kLoop, calls=%fused_computation.5 | loop fusion | flops 6192704 | bytes 4130560 | tf_op jit(solution)/shard_map/reduce_sum | solution.py:74
  233.1 0.2 copy-done.1
  233.3 0.8 convert_reduce_fusion
  234.1 4.3 %select_reduce_fusion = (f32[448]{0:T(512)S(1)}, f32[448]{0:T(512)S(1)}, f32[448,384]{1,0:T(8,128)}) fusion(s32[448]{0:T(512)S(1)} %broadcast_subtract_fusion.1, bf16[4608,384]{1,0:T(8,128)(2,1)S(1)} %bitcast.11, f32[448]{0:T(512)S(1)} %add_rsqrt_fusion, f32[4608]{0:T(1024)S(1)} %convert_reduce_fusion, bf16[4608,449]{1,0:T(8,128)(2,1)S(1)} %copy-done.1), kind=kOutput, calls=%fused_computation.15 | convolution fusion | flops 1594735616 | bytes 8390656 | tf_op jit(solution)/shard_map/dot_general | solution.py:79
  238.4 8.3 %all-reduce.1 = (f32[448]{0:T(512)S(1)}, f32[448]{0:T(512)S(1)}) all-reduce(f32[448]{0:T(512)S(1)} %get-tuple-element.16, f32[448]{0:T(512)S(1)} %get-tuple-element.15), channel_id=1, replica_groups=mesh['group_0'=4,'group_1'=2,'vocab_0'=16,'vocab_1'=2,'vocab_2'=2] {'gro..., use_global_device_ids=true, to_apply=%region_3.4 | all-reduce | flops 896 | bytes 7168 | tf_op jit(solution)/shard_map/psum | solution.py:55
  246.8 5.5 %all-reduce.4 = (f32[448]{0:T(512)S(1)}, f32[448]{0:T(512)S(1)}) all-reduce(f32[448]{0:T(512)S(1)} %get-tuple-element.19, f32[448]{0:T(512)S(1)} %get-tuple-element.20), channel_id=1, replica_groups=mesh['group_0'=4,'group_1'=2,'vocab_0'=16,'vocab_1'=2,'vocab_2'=2] {'gro..., use_global_device_ids=true, to_apply=%region_4.5 | all-reduce | flops 896 | bytes 7168 | tf_op jit(solution)/shard_map/psum | solution.py:55
  252.3 22.0 %all-reduce = (f32[448]{0:T(512)S(1)}, f32[448]{0:T(512)S(1)}) all-reduce(f32[448]{0:T(512)S(1)} %get-tuple-element.25, f32[448]{0:T(512)S(1)} %get-tuple-element.26), channel_id=1, replica_groups=mesh['group_0'=4,'group_1'=2,'vocab_0'=16,'vocab_1'=2,'vocab_2'=2] {'voc..., use_global_device_ids=true, to_apply=%region_5.6 | all-reduce | flops 896 | bytes 7168 | tf_op jit(solution)/shard_map/psum | solution.py:55
  274.3 3.8 %all-reduce.3 = (f32[448]{0:T(512)S(1)}, f32[448]{0:T(512)S(1)}) all-reduce(f32[448]{0:T(512)S(1)} %get-tuple-element.17, f32[448]{0:T(512)S(1)} %get-tuple-element.18), channel_id=1, replica_groups=mesh['group_0'=4,'group_1'=2,'vocab_0'=16,'vocab_1'=2,'vocab_2'=2] {'voc..., use_global_device_ids=true, to_apply=%region_6.7 | all-reduce | flops 896 | bytes 7168 | tf_op jit(solution)/shard_map/psum | solution.py:55
  278.1 13.8 %all-reduce.2 = (f32[448]{0:T(512)S(1)}, f32[448]{0:T(512)S(1)}) all-reduce(f32[448]{0:T(512)S(1)} %get-tuple-element.23, f32[448]{0:T(512)S(1)} %get-tuple-element.24), channel_id=1, replica_groups=mesh['group_0'=4,'group_1'=2,'vocab_0'=16,'vocab_1'=2,'vocab_2'=2] {'voc..., use_global_device_ids=true, to_apply=%region_7.8 | all-reduce | flops 896 | bytes 7168 | tf_op jit(solution)/shard_map/psum | solution.py:55
  291.9 0.6 log_subtract_fusion
  292.5 2.1 broadcast_subtract_fusion
  (5 shorter events, 0.1 us)
Async XLA Ops:
  9.9 20.6 %copy-start.3 = (bf16[72]{0:T(256)(128)(2,1)S(1)}, bf16[72]{0:T(256)(128)(2,1)}, u32[]{:S(2)}) copy-start(bf16[72]{0:T(256)(128)(2,1)} %param.6) | copy-start | bytes 436
  12.2 103.1 %all-to-all-start = ((bf16[64,32,384]{2,1,0:T(8,128)(2,1)}), bf16[64,32,384]{2,1,0:T(8,128)(2,1)}, u32[]{:S(2)}, u32[]{:S(2)}) async-start(bf16[64,32,384]{2,1,0:T(8,128)(2,1)} %copy.19), calls=%async_computation | async-start | bytes 3145728 | tf_op jit(solution)/shard_map/all_to_all | solution.py:49
  30.5 199.0 %all-gather.2.cloned.1.call-start = ((), (), s32[]{:S(2)}) async-start(), calls=%async_computation.2 | async-start | bytes 4792320 | tf_op jit(solution)/shard_map/all_gather | solution.py:17
  33.1 89.0 %copy-start = (bf16[72,24576]{1,0:T(8,128)(2,1)S(1)}, bf16[72,24576]{1,0:T(8,128)(2,1)}, u32[]{:S(2)}) copy-start(bf16[72,24576]{1,0:T(8,128)(2,1)} %param.4) | copy-start | bytes 10616836
  115.3 111.9 %all-to-all-start.1 = ((bf16[64,40,384]{2,1,0:T(8,128)(2,1)}), bf16[64,40,384]{2,1,0:T(8,128)(2,1)}, u32[]{:S(2)}, u32[]{:S(2)}) async-start(bf16[64,40,384]{2,1,0:T(8,128)(2,1)} %copy.20), calls=%async_computation.1 | async-start | bytes 3932160 | tf_op jit(solution)/shard_map/all_to_all | solution.py:49
  122.1 5.3 %copy-start.2 = (s32[448]{0:T(512)S(1)}, s32[448]{0:T(512)}, u32[]{:S(2)}) copy-start(s32[448]{0:T(512)} %param.7) | copy-start | bytes 5380
  229.5 3.8 %copy-start.1 = (bf16[4608,449]{1,0:T(8,128)(2,1)S(1)}, bf16[4608,449]{1,0:T(8,128)(2,1)}, u32[]{:S(2)}) copy-start(bf16[4608,449]{1,0:T(8,128)(2,1)} %all-gather.2.cloned.1.call-done) | copy-start | bytes 12413956
Sparse Core Ops, SparseCore 0:
  34.0 191.4 all-gather.1
where the time goes:
time: 302 us; the launch traced here: 301 us
  waiting for transfers between devices  135 us (45%)
  blocking collectives  92.1 us (30%)
  starting transfers between devices  25.2 us (8%)
  local copies, waits for them, and re-layouts  19.4 us (6%)
  between operations  14.2 us (5%)
  other arithmetic  11.3 us (4%)
  matrix products  4.32 us (1%)
    all_to_all x2, waiting for transfers between devices, several_exchanges(): lax.all_to_all(slab, axis, split_axis=0, concat_axis=0, tiled=True)  135 us
    psum x5, blocking collectives, over_axes(): array = lax.psum(array, axis)  53.4 us
    psum x1, blocking collectives, body(): embed_cols = lax.psum(found.astype(jnp.bfloat16), GROUP).astype(jnp.float32)  38.7 us
    all_to_all x2, starting transfers between devices, several_exchanges(): lax.all_to_all(slab, axis, split_axis=0, concat_axis=0, tiled=True)  25.1 us
    unnamed x11, local copies, waits for them, and re-layouts  8.96 us
  transfers between devices with their start and end apart: 3, of which 2 were waited for; matrix products, arithmetic and copies ran while one was open for 6% of the time, Pallas kernels for 0%

commit v1 on v0

v1 whole, which is shorter than its diff:
```python
import math

import jax
import jax.numpy as jnp
from jax import lax
from jax.experimental import pallas as pl
from jax.experimental.pallas import tpu as pltpu
from jax.sharding import Mesh
from jax.sharding import PartitionSpec as P

GROUP = ("group_0", "group_1")
FAR = "depth"
NEAR = ("row", "core")
VOCAB = (FAR,) + NEAR
PLANE = GROUP + NEAR
LANES = 512


def copies_of(x, axes):
    many = jnp.broadcast_to(x[None], (lax.axis_size(axes),) + x.shape)
    return lax.all_to_all(many, axes, split_axis=0, concat_axis=0, tiled=True)


def as_rows(x):
    return jnp.pad(x, (0, LANES - x.shape[0])).reshape(LANES // 128, 128)


def arrange(table, places, near_index, near_n):
    share, span_cols = table.shape
    slots = places.shape[0]
    cols = span_cols // (lax.axis_size(FAR) * near_n)

    def kernel(places_ref, near_ref, table_ref, *refs):
        out_refs, sems = refs[:near_n], refs[near_n]
        copies = []
        for k in range(near_n):
            for j in range(slots):
                block = places_ref[j] * near_n + (near_ref[0] ^ k)
                copies.append(
                    pltpu.make_async_copy(
                        table_ref.at[:, pl.ds(pl.multiple_of(block * cols, cols), cols)],
                        out_refs[k].at[:, pl.ds(j * cols, cols)],
                        sems.at[k * slots + j],
                    )
                )
        for c in copies:
            c.start()
        for c in copies:
            c.wait()

    smem, vmem = pl.BlockSpec(memory_space=pltpu.SMEM), pl.BlockSpec(memory_space=pltpu.VMEM)
    return pl.pallas_call(
        kernel,
        in_specs=[smem, smem, pl.BlockSpec(memory_space=pltpu.HBM)],
        out_specs=[vmem] * near_n,
        out_shape=[jax.ShapeDtypeStruct((share, slots * cols), table.dtype)] * near_n,
        scratch_shapes=[pltpu.SemaphoreType.DMA((near_n * slots,))],
    )(places, near_index[None], table)


def add_partial(x, w, slot, cols, received, dtype):
    y = jnp.dot(x, w[:, slot * cols : (slot + 1) * cols], preferred_element_type=jnp.float32)
    for r in received:
        y = y + r.astype(jnp.float32)
    return y.astype(dtype)


def layer(table, hidden, gain, ids):
    share, span_cols = table.shape
    tok = hidden.shape[0]
    far_n, near_n = lax.axis_size(FAR), lax.axis_size(NEAR)
    voc_cols = span_cols // (far_n * near_n)
    width = share * far_n * near_n
    group_index = lax.axis_index(GROUP)
    vocab_index = lax.axis_index(VOCAB)
    depth = lax.axis_index(FAR)
    steps = far_n // 2

    order = []
    for s in range(steps):
        order += [steps - s, (s - steps + 1)]
    places = (depth + jnp.array(order, jnp.int32)) % far_n
    early = far_n // 2

    fill = jnp.broadcast_to(gain[:, None], (share, LANES - tok))
    both = jnp.concatenate([hidden.T, fill], axis=1)
    near_index = lax.axis_index(NEAR)
    first = arrange(table, places[:early], near_index, near_n)
    both = lax.all_gather(both, NEAR, axis=0, tiled=True)
    first, both = lax.optimization_barrier((first, both))
    swapped = jnp.zeros((near_n * share, first[0].shape[1]), table.dtype)
    for k in range(near_n):
        slab = first[k]
        if k:
            slab = lax.ppermute(slab, NEAR, [(i, i ^ k) for i in range(near_n)])
        swapped = lax.dynamic_update_slice(swapped, slab, ((near_index ^ k) * share, 0))
    first = swapped

    both = both.astype(jnp.float32)
    states, gains = both[:, :tok], both[:, tok : tok + 1]
    squares = jnp.sum(states * states, axis=0)
    squares, late_table = lax.optimization_barrier((squares, table))
    squares = copies_of(as_rows(squares), FAR).reshape(far_n, -1, 128)
    mean_sq = squares.sum(axis=0).reshape(LANES)[:tok] / width
    normed = (states * gains * lax.rsqrt(mean_sq + 1e-06)[None, :]).astype(jnp.bfloat16).T

    second = arrange(late_table, places[early:], near_index * 0, near_n)
    second = jnp.stack(second)
    second = lax.all_to_all(second, NEAR, split_axis=0, concat_axis=0, tiled=True)
    second = second.reshape(near_n * share, -1)

    def part(slot, received, dtype=jnp.bfloat16):
        w, at = (first, slot) if slot < early else (second, slot - early)
        return add_partial(normed, w, at, voc_cols, received, dtype)

    ahead = [(i, (i + 1) % far_n) for i in range(far_n)]
    behind = [(i, (i - 1) % far_n) for i in range(far_n)]
    up, down = [], []
    for s in range(steps):
        out = part(2 * s, up)
        up = [lax.ppermute(out, FAR, ahead)]
        if s < steps - 1:
            out = part(2 * s + 1, down)
            down = [lax.ppermute(out, FAR, behind)]
    logits = part(2 * steps - 1, up + down, jnp.float32)

    local_ids = ids - group_index * span_cols
    inside = jnp.logical_and(local_ids >= 0, local_ids < span_cols)
    found = jnp.take(late_table, jnp.clip(local_ids, 0, span_cols - 1), axis=1)
    found = jnp.where(inside[None, :], found, 0)
    found = copies_of(found, GROUP).reshape(-1, share, tok)
    embed = jnp.sum(found.astype(jnp.float32), axis=0)
    next_embed = (embed * math.sqrt(width)).astype(jnp.bfloat16).T

    capped = 30.0 * jnp.tanh(logits / 30.0)
    offsets = ids - (group_index * far_n * near_n + vocab_index) * voc_cols
    columns = lax.broadcasted_iota(jnp.int32, capped.shape, 1)
    pick = jnp.sum(jnp.where(columns == offsets[:, None], capped, 0.0), axis=1)
    sums = jnp.sum(jnp.exp(capped), axis=1)
    pair = jnp.concatenate([as_rows(sums), as_rows(pick)])
    for axes in (PLANE, FAR):
        pair = copies_of(pair, axes).reshape(-1, *pair.shape).sum(axis=0)
    totals, picks = pair.reshape(2, LANES)[:, :tok]
    log_total = jnp.log(totals)
    return (next_embed, capped - log_total[:, None], picks - log_total)


def solution(mesh):
    torus = Mesh(
        mesh.devices.reshape(4, 2, 16, 2, 2),
        GROUP + VOCAB,
    )
    return jax.shard_map(
        layer,
        mesh=torus,
        in_specs=(P(VOCAB, GROUP), P(None, VOCAB), P(VOCAB), P()),
        out_specs=(P(None, VOCAB), P(None, GROUP + VOCAB), P()),
        check_vma=False,
    )
```

time: 302 us -> 209 us (0.69)
  waiting for transfers between devices: 135 us -> 48.3 us
  blocking collectives: 92.1 us -> 12.5 us
  starting transfers between devices: 25.2 us -> 95.1 us
  between operations: 14.2 us -> 1.35 us
  matrix products: 4.32 us -> 16.4 us
  Pallas kernels: 0 us -> 7.24 us
    all_to_all x2 -> x5, waiting for transfers between devices: 135 us -> 35.8 us  [the longest x4 35.8 us: copies_of(): return lax.all_to_all(many, axes, split_axis=0, concat_axis=0, tiled=True)]
    psum x6 -> x0, blocking collectives: 92.1 us -> none  [the longest x5 53.4 us: over_axes(): array = lax.psum(array, axis)]
    ppermute x0 -> x18, starting transfers between devices: none -> 59.1 us  [the longest x7 35.2 us: layer(): down = [lax.ppermute(out, FAR, behind)]]
    all_gather x0 -> x1, blocking collectives: none -> 12.5 us  [layer(): both = lax.all_gather(both, NEAR, axis=0, tiled=True)]
    ppermute x0 -> x18, waiting for transfers between devices: none -> 12.5 us  [the longest x7 9.23 us: layer(): down = [lax.ppermute(out, FAR, behind)]]
    dot_general x1 -> x16, matrix products: 4.32 us -> 16.4 us  [add_partial(): jnp.dot(x, w[:, slot * cols:(slot + 1) * cols], preferred_element_type=jn...]
    all_to_all x2 -> x5, starting transfers between devices: 25.1 us -> 36 us  [the longest x4 30.9 us: copies_of(): return lax.all_to_all(many, axes, split_axis=0, concat_axis=0, tiled=True)]
    unnamed x11 -> x22, local copies, waits for them, and re-layouts: 8.96 us -> 0.85 us
  transfers between devices with their start and end apart: 3 -> 23, of which waited for: 2 -> 13; matrix products, arithmetic and copies ran while one was open for 6% -> 15% of each run, Pallas kernels for 0% -> 2%
where the time goes in v1:
time: 209 us; the launch traced here: 207 us
  starting transfers between devices  95.1 us (46%)
  waiting for transfers between devices  48.3 us (23%)
  local copies, waits for them, and re-layouts  16.8 us (8%)
  matrix products  16.4 us (8%)
  blocking collectives  12.5 us (6%)
  other arithmetic  9.03 us (4%)
  Pallas kernels  7.24 us (3%)
    all_to_all x4, waiting for transfers between devices, copies_of(): return lax.all_to_all(many, axes, split_axis=0, concat_axis=0, tiled=True)  35.8 us
    ppermute x7, starting transfers between devices, layer(): down = [lax.ppermute(out, FAR, behind)]  35.2 us
    all_to_all x4, starting transfers between devices, copies_of(): return lax.all_to_all(many, axes, split_axis=0, concat_axis=0, tiled=True)  30.9 us
    dot_general x16, matrix products, add_partial(): jnp.dot(x, w[:, slot * cols:(slot + 1) * cols], preferred_element_type=jn...  16.4 us
    ppermute x8, starting transfers between devices, layer(): up = [lax.ppermute(out, FAR, ahead)]  16 us
    all_gather x1, blocking collectives, layer(): both = lax.all_gather(both, NEAR, axis=0, tiled=True)  12.5 us
    ppermute x7, waiting for transfers between devices, layer(): down = [lax.ppermute(out, FAR, behind)]  9.23 us
    ppermute x3, starting transfers between devices, layer(): slab = lax.ppermute(slab, NEAR, [(i, i ^ k) for i in range(near_n)])  7.87 us
  transfers between devices with their start and end apart: 23, of which 13 were waited for; matrix products, arithmetic and copies ran while one was open for 15% of the time, Pallas kernels for 2%

profile of v1, /device:TPU:1, one launch (start us, length us, event | category | flops | bytes accessed | tf_op | source)
XLA Modules:
  0.0 206.8 jit_solution(1639249717438252270)
XLA Ops:
  0.6 0.7 and_select_fusion
  1.3 0.6 fusion.33
  1.9 0.7 broadcast_in_dim.72
  2.6 1.0 pad_maximum_fusion.1
  3.6 12.5 %all_gather.3 = bf16[288,512]{1,0:T(8,128)(2,1)S(1)} all-gather(bf16[72,512]{1,0:T(8,128)(2,1)S(1)} %pad_maximum_fusion.1), channel_id=1, replica_groups=mesh['group_0'=4,'group_1'=2,'depth'=16,'row'=2,'core'=2] {'row','core'}, dimensions={0}, use_global_device_ids=true | all-gather | bytes 368640 | tf_op jit(solution)/shard_map/all_gather | solution.py:89
  16.1 3.6 %shard_map.76 = (bf16[72,3072]{1,0:T(8,128)(2,1)}, bf16[72,3072]{1,0:T(8,128)(2,1)}, bf16[72,3072]{1,0:T(8,128)(2,1)}, bf16[72,3072]{1,0:T(8,128)(2,1)}) custom-call(s32[8]{0:T(128)} %get-tuple-element.41.places_ref, s32[1]{0:T(128)} %bitcast.near_ref, bf16[72,24576]{1,0:T(8,128)(2,1)} %table_ref.2), custom_call_target="tpu_custom_call" | custom-call | tf_op jit(solution)/shard_map/pallas_call | solution.py:52
  19.7 2.1 %collective-permute-start = (bf16[72,3072]{1,0:T(8,128)(2,1)}, bf16[72,3072]{1,0:T(8,128)(2,1)}, u32[]{:S(2)}, u32[]{:S(2)}) collective-permute-start(bf16[72,3072]{1,0:T(8,128)(2,1)} %get-tuple-element.30), channel_id=1, source_target_pairs={{0,1},{1,0},{2,3},{3,2},{4,5},{5,4},{6,7},{7,6},{8,9},{9,8},{10,11... | collective-permute-start | bytes 1327112 | tf_op jit(solution)/shard_map/ppermute | solution.py:95
  21.8 2.2 %collective-permute-start.1 = (bf16[72,3072]{1,0:T(8,128)(2,1)}, bf16[72,3072]{1,0:T(8,128)(2,1)S(1)}, u32[]{:S(2)}, u32[]{:S(2)}) collective-permute-start(bf16[72,3072]{1,0:T(8,128)(2,1)} %get-tuple-element.31), channel_id=1, source_target_pairs={{0,2},{1,3},{2,0},{3,1},{4,6},{5,7},{6,4},{7,5},{8,10},{9,11},{10,... | collective-permute-start | bytes 1327112 | tf_op jit(solution)/shard_map/ppermute | solution.py:95
  24.1 3.6 %collective-permute-start.2 = (bf16[72,3072]{1,0:T(8,128)(2,1)}, bf16[72,3072]{1,0:T(8,128)(2,1)S(1)}, u32[]{:S(2)}, u32[]{:S(2)}) collective-permute-start(bf16[72,3072]{1,0:T(8,128)(2,1)} %get-tuple-element.32), channel_id=1, source_target_pairs={{0,3},{1,2},{2,1},{3,0},{4,7},{5,6},{6,5},{7,4},{8,11},{9,10},{10,... | collective-permute-start | bytes 1327112 | tf_op jit(solution)/shard_map/ppermute | solution.py:95
  27.8 0.6 broadcast_in_dim.78
  28.4 9.7 %all-to-all-start.1 = ((f32[16,4,128]{2,1,0:T(4,128)}), f32[16,4,128]{2,1,0:T(4,128)S(1)}, u32[]{:S(2)}, u32[]{:S(2)}) async-start(f32[16,4,128]{2,1,0:T(4,128)} %broadcast_in_dim.78), calls=%async_computation.1 | async-start | bytes 65536 | tf_op jit(solution)/shard_map/all_to_all | solution.py:21
  38.3 0.8 copy-done.9
  39.2 3.6 %shard_map.77 = (bf16[72,3072]{1,0:T(8,128)(2,1)}, bf16[72,3072]{1,0:T(8,128)(2,1)}, bf16[72,3072]{1,0:T(8,128)(2,1)}, bf16[72,3072]{1,0:T(8,128)(2,1)}) custom-call(s32[8]{0:T(128)} %get-tuple-element.40.places_ref, s32[1]{0:T(128)} %constant.83.clone.1.near_ref, bf16[72,24576]{1,0:T(8,128)(2,1)} %table_ref.2), custom_call_target="tpu_custom_call" | custom-call | tf_op jit(solution)/shard_map/pallas_call | solution.py:52
  43.1 6.6 %all-to-all-done.1 = f32[16,4,128]{2,1,0:T(4,128)S(1)} async-done(((f32[16,4,128]{2,1,0:T(4,128)}), f32[16,4,128]{2,1,0:T(4,128)S(1)}, u32[]{:S(2)}, u32[]{:S(2)}) %all-to-all-start.1) | async-done | bytes 32800 | tf_op jit(solution)/shard_map/all_to_all | solution.py:21
  49.8 1.2 constant_dynamic-update-slice_fusion.2
  51.6 2.4 %collective-permute-start.3 = (bf16[448,384]{1,0:T(8,128)(2,1)S(1)}, bf16[448,384]{1,0:T(8,128)(2,1)S(1)}, u32[]{:S(2)}, u32[]{:S(2)}) collective-permute-start(bf16[448,384]{1,0:T(8,128)(2,1)S(1)} %convolution_convert_fusion.1), channel_id=1, source_target_pairs={{0,4},{4,8},{8,12},{12,16},{16,20},{20,24},{24,28},{28,32},{32,36}... | collective-permute-start | bytes 1032200 | tf_op jit(solution)/shard_map/ppermute | solution.py:121
  54.0 1.4 pad_maximum_fusion
  55.4 5.1 %all-to-all-start.2 = ((bf16[4,72,3072]{2,1,0:T(8,128)(2,1)}), bf16[4,72,3072]{2,1,0:T(8,128)(2,1)S(1)}, u32[]{:S(2)}, u32[]{:S(2)}) async-start(bf16[4,72,3072]{2,1,0:T(8,128)(2,1)} %pad_maximum_fusion), calls=%async_computation.2 | async-start | bytes 3538944 | tf_op jit(solution)/shard_map/all_to_all | solution.py:109
  60.6 1.3 convolution_convert_fusion
  61.9 4.2 %collective-permute-start.11 = (bf16[448,384]{1,0:T(8,128)(2,1)S(1)}, bf16[448,384]{1,0:T(8,128)(2,1)S(1)}, u32[]{:S(2)}, u32[]{:S(2)}) collective-permute-start(bf16[448,384]{1,0:T(8,128)(2,1)S(1)} %convolution_convert_fusion), channel_id=1, source_target_pairs={{0,60},{4,0},{8,4},{12,8},{16,12},{20,16},{24,20},{28,24},{32,28},... | collective-permute-start | bytes 1032200 | tf_op jit(solution)/shard_map/ppermute | solution.py:124
  66.2 1.3 fusion.2
  67.5 1.9 collective-permute-start.4
  69.4 4.1 %collective-permute-done.11 = bf16[448,384]{1,0:T(8,128)(2,1)S(1)} collective-permute-done((bf16[448,384]{1,0:T(8,128)(2,1)S(1)}, bf16[448,384]{1,0:T(8,128)(2,1)S(1)}, u32[]{:S(2)}, u32[]{:S(2)}) %collective-permute-start.11) | collective-permute-done | bytes 344096 | tf_op jit(solution)/shard_map/ppermute | solution.py:124
  73.5 1.3 fusion.5
  74.8 5.3 %collective-permute-start.12 = (bf16[448,384]{1,0:T(8,128)(2,1)S(1)}, bf16[448,384]{1,0:T(8,128)(2,1)S(1)}, u32[]{:S(2)}, u32[]{:S(2)}) collective-permute-start(bf16[448,384]{1,0:T(8,128)(2,1)S(1)} %fusion.5), channel_id=1, source_target_pairs={{0,60},{4,0},{8,4},{12,8},{16,12},{20,16},{24,20},{28,24},{32,28},... | collective-permute-start | bytes 1032200 | tf_op jit(solution)/shard_map/ppermute | solution.py:124
  80.2 2.1 %fusion.1 = bf16[448,384]{1,0:T(8,128)(2,1)} fusion(bf16[288,448]{1,0:T(8,128)(2,1)S(1)} %multiply_convert_fusion, bf16[448,384]{1,0:T(8,128)(2,1)S(1)} %collective-permute-done.4, bf16[288,3072]{1,0:T(8,128)(2,1)} %copy-done.4), kind=kOutput, calls=%fused_computation.9 | convolution fusion | flops 99606528 | bytes 1167360 | tf_op jit(solution)/shard_map/dot_general | solution.py:62
  82.3 1.9 collective-permute-start.5
  84.2 2.5 %collective-permute-done.12 = bf16[448,384]{1,0:T(8,128)(2,1)S(1)} collective-permute-done((bf16[448,384]{1,0:T(8,128)(2,1)S(1)}, bf16[448,384]{1,0:T(8,128)(2,1)S(1)}, u32[]{:S(2)}, u32[]{:S(2)}) %collective-permute-start.12) | collective-permute-done | bytes 344096 | tf_op jit(solution)/shard_map/ppermute | solution.py:124
  86.7 1.3 fusion.4
  88.0 5.3 %collective-permute-start.13 = (bf16[448,384]{1,0:T(8,128)(2,1)S(1)}, bf16[448,384]{1,0:T(8,128)(2,1)S(1)}, u32[]{:S(2)}, u32[]{:S(2)}) collective-permute-start(bf16[448,384]{1,0:T(8,128)(2,1)S(1)} %fusion.4), channel_id=1, source_target_pairs={{0,60},{4,0},{8,4},{12,8},{16,12},{20,16},{24,20},{28,24},{32,28},... | collective-permute-start | bytes 1032200 | tf_op jit(solution)/shard_map/ppermute | solution.py:124
  94.6 1.5 fusion
  96.1 1.9 collective-permute-start.6
  99.0 1.3 fusion.3
  100.3 5.3 %collective-permute-start.14 = (bf16[448,384]{1,0:T(8,128)(2,1)S(1)}, bf16[448,384]{1,0:T(8,128)(2,1)S(1)}, u32[]{:S(2)}, u32[]{:S(2)}) collective-permute-start(bf16[448,384]{1,0:T(8,128)(2,1)S(1)} %fusion.3), channel_id=1, source_target_pairs={{0,60},{4,0},{8,4},{12,8},{16,12},{20,16},{24,20},{28,24},{32,28},... | collective-permute-start | bytes 1032200 | tf_op jit(solution)/shard_map/ppermute | solution.py:124
  105.6 1.1 collective-permute-done.6
  106.8 1.9 collective-permute-start.7
  109.2 1.2 collective-permute-done.14
  110.5 5.3 %collective-permute-start.15 = (bf16[448,384]{1,0:T(8,128)(2,1)S(1)}, bf16[448,384]{1,0:T(8,128)(2,1)S(1)}, u32[]{:S(2)}, u32[]{:S(2)}) collective-permute-start(bf16[448,384]{1,0:T(8,128)(2,1)S(1)} %add_convert_fusion.2), channel_id=1, source_target_pairs={{0,60},{4,0},{8,4},{12,8},{16,12},{20,16},{24,20},{28,24},{32,28},... | collective-permute-start | bytes 1032200 | tf_op jit(solution)/shard_map/ppermute | solution.py:124
  115.8 0.9 collective-permute-done.7
  116.7 1.9 collective-permute-start.8
  119.1 0.9 collective-permute-done.15
  120.0 5.0 %collective-permute-start.16 = (bf16[448,384]{1,0:T(8,128)(2,1)S(1)}, bf16[448,384]{1,0:T(8,128)(2,1)S(1)}, u32[]{:S(2)}, u32[]{:S(2)}) collective-permute-start(bf16[448,384]{1,0:T(8,128)(2,1)S(1)} %add_convert_fusion.1), channel_id=1, source_target_pairs={{0,60},{4,0},{8,4},{12,8},{16,12},{20,16},{24,20},{28,24},{32,28},... | collective-permute-start | bytes 1032200 | tf_op jit(solution)/shard_map/ppermute | solution.py:124
  125.1 0.9 collective-permute-done.8
  126.0 2.2 %collective-permute-start.9 = (bf16[448,384]{1,0:T(8,128)(2,1)S(1)}, bf16[448,384]{1,0:T(8,128)(2,1)S(1)}, u32[]{:S(2)}, u32[]{:S(2)}) collective-permute-start(bf16[448,384]{1,0:T(8,128)(2,1)S(1)} %add_convert_fusion.4), channel_id=1, source_target_pairs={{0,4},{4,8},{8,12},{12,16},{16,20},{20,24},{24,28},{28,32},{32,36}... | collective-permute-start | bytes 1032200 | tf_op jit(solution)/shard_map/ppermute | solution.py:121
  128.2 1.3 fusion.14
  129.6 0.8 add_convert_fusion
  130.4 4.7 %collective-permute-start.17 = (bf16[448,384]{1,0:T(8,128)(2,1)}, bf16[448,384]{1,0:T(8,128)(2,1)}, u32[]{:S(2)}, u32[]{:S(2)}) collective-permute-start(bf16[448,384]{1,0:T(8,128)(2,1)} %add_convert_fusion), channel_id=1, source_target_pairs={{0,60},{4,0},{8,4},{12,8},{16,12},{20,16},{24,20},{28,24},{32,28},... | collective-permute-start | bytes 1032200 | tf_op jit(solution)/shard_map/ppermute | solution.py:124
  135.5 0.8 add_convert_fusion.3
  136.3 1.9 collective-permute-start.10
  138.3 5.3 %copy.14 = bf16[72,24576]{0,1:T(8,128)(2,1)} copy(bf16[72,24576]{1,0:T(8,128)(2,1)S(1)} %copy-done) | data formatting | bytes 7077888 | tf_op jit(solution)/shard_map/optimization_barrier | solution.py:102
  143.5 4.8 %gather_fusion = bf16[448,72]{1,0:T(8,128)(2,1)S(1)} fusion(bf16[72,24576]{0,1:T(8,128)(2,1)} %copy.14, s32[1024]{0:T(1024)S(1)} %pad_clamp_fusion), kind=kCustom, calls=%fused_computation | custom fusion | bytes 130816 | tf_op jit(solution)/shard_map/jit(_take)/gather | solution.py:129
  148.4 2.1 exponential_reduce_fusion
  150.5 0.7 broadcast_in_dim.81
  151.1 13.0 %all-to-all-start.3 = ((f32[32,8,128]{2,1,0:T(8,128)}), f32[32,8,128]{2,1,0:T(8,128)S(1)}, u32[]{:S(2)}, u32[]{:S(2)}) async-start(f32[32,8,128]{2,1,0:T(8,128)} %broadcast_in_dim.81), calls=%async_computation.3 | async-start | bytes 262144 | tf_op jit(solution)/shard_map/all_to_all | solution.py:21
  164.4 7.4 %all-to-all-done.3 = f32[32,8,128]{2,1,0:T(8,128)S(1)} async-done(((f32[32,8,128]{2,1,0:T(8,128)}), f32[32,8,128]{2,1,0:T(8,128)S(1)}, u32[]{:S(2)}, u32[]{:S(2)}) %all-to-all-start.3) | async-done | bytes 131104 | tf_op jit(solution)/shard_map/all_to_all | solution.py:21
  171.8 0.9 broadcast_in_dim.76
  172.6 3.5 %all-to-all-start = ((bf16[8,72,448]{2,1,0:T(8,128)(2,1)}), bf16[8,72,448]{2,1,0:T(8,128)(2,1)S(1)}, u32[]{:S(2)}, u32[]{:S(2)}) async-start(bf16[8,72,448]{2,1,0:T(8,128)(2,1)} %broadcast_in_dim.76), calls=%async_computation | async-start | bytes 1179648 | tf_op jit(solution)/shard_map/all_to_all | solution.py:21
  176.2 11.0 %all-to-all-done = bf16[8,72,448]{2,1,0:T(8,128)(2,1)S(1)} async-done(((bf16[8,72,448]{2,1,0:T(8,128)(2,1)}), bf16[8,72,448]{2,1,0:T(8,128)(2,1)S(1)}, u32[]{:S(2)}, u32[]{:S(2)}) %all-to-all-start) | async-done | bytes 516128 | tf_op jit(solution)/shard_map/all_to_all | solution.py:21
  187.2 0.6 broadcast_in_dim.82
  187.9 4.6 %all-to-all-start.4 = ((f32[16,8,128]{2,1,0:T(8,128)}), f32[16,8,128]{2,1,0:T(8,128)S(1)}, u32[]{:S(2)}, u32[]{:S(2)}) async-start(f32[16,8,128]{2,1,0:T(8,128)} %broadcast_in_dim.82), calls=%async_computation.4 | async-start | bytes 131072 | tf_op jit(solution)/shard_map/all_to_all | solution.py:21
  192.6 0.6 fusion.30
  193.2 10.8 %all-to-all-done.4 = f32[16,8,128]{2,1,0:T(8,128)S(1)} async-done(((f32[16,8,128]{2,1,0:T(8,128)}), f32[16,8,128]{2,1,0:T(8,128)S(1)}, u32[]{:S(2)}, u32[]{:S(2)}) %all-to-all-start.4) | async-done | bytes 65568 | tf_op jit(solution)/shard_map/all_to_all | solution.py:21
  204.1 0.6 sub.29
  204.7 2.1 %broadcast_subtract_fusion = f32[448,384]{1,0:T(8,128)} fusion(f32[448]{0:T(512)S(1)} %bitcast.50, bf16[448,384]{1,0:T(8,128)(2,1)} %collective-permute-done.17, f32[448,384]{1,0:T(8,128)S(1)} %get-tuple-element.42, bf16[448,384]{1,0:T(8,128)(2,1)} %collective-permute-done.10), kind=kLoop, calls=%fused_computation.30 | loop fusion | flops 1204224 | bytes 2066176 | tf_op jit(solution)/shard_map/sub | solution.py:145
  (68 shorter events, 5.5 us)
Async XLA Ops:
  19.7 30.1 %collective-permute-start = (bf16[72,3072]{1,0:T(8,128)(2,1)}, bf16[72,3072]{1,0:T(8,128)(2,1)}, u32[]{:S(2)}, u32[]{:S(2)}) collective-permute-start(bf16[72,3072]{1,0:T(8,128)(2,1)} %get-tuple-element.30), channel_id=1, source_target_pairs={{0,1},{1,0},{2,3},{3,2},{4,5},{5,4},{6,7},{7,6},{8,9},{9,8},{10,11... | collective-permute-start | bytes 1327112 | tf_op jit(solution)/shard_map/ppermute | solution.py:95
  21.8 29.2 %collective-permute-start.1 = (bf16[72,3072]{1,0:T(8,128)(2,1)}, bf16[72,3072]{1,0:T(8,128)(2,1)S(1)}, u32[]{:S(2)}, u32[]{:S(2)}) collective-permute-start(bf16[72,3072]{1,0:T(8,128)(2,1)} %get-tuple-element.31), channel_id=1, source_target_pairs={{0,2},{1,3},{2,0},{3,1},{4,6},{5,7},{6,4},{7,5},{8,10},{9,11},{10,... | collective-permute-start | bytes 1327112 | tf_op jit(solution)/shard_map/ppermute | solution.py:95
  24.1 27.0 %collective-permute-start.2 = (bf16[72,3072]{1,0:T(8,128)(2,1)}, bf16[72,3072]{1,0:T(8,128)(2,1)S(1)}, u32[]{:S(2)}, u32[]{:S(2)}) collective-permute-start(bf16[72,3072]{1,0:T(8,128)(2,1)} %get-tuple-element.32), channel_id=1, source_target_pairs={{0,3},{1,2},{2,1},{3,0},{4,7},{5,6},{6,5},{7,4},{8,11},{9,10},{10,... | collective-permute-start | bytes 1327112 | tf_op jit(solution)/shard_map/ppermute | solution.py:95
  28.4 21.2 %all-to-all-start.1 = ((f32[16,4,128]{2,1,0:T(4,128)}), f32[16,4,128]{2,1,0:T(4,128)S(1)}, u32[]{:S(2)}, u32[]{:S(2)}) async-start(f32[16,4,128]{2,1,0:T(4,128)} %broadcast_in_dim.78), calls=%async_computation.1 | async-start | bytes 65536 | tf_op jit(solution)/shard_map/all_to_all | solution.py:21
  38.1 1.0 copy-start.9
  49.8 68.9 %copy-start.1 = (bf16[288,448]{1,0:T(8,128)(2,1)}, bf16[288,448]{1,0:T(8,128)(2,1)S(1)}, u32[]{:S(2)}) copy-start(bf16[288,448]{1,0:T(8,128)(2,1)S(1)} %multiply_convert_fusion) | copy-start | bytes 774148
  49.8 4.1 %copy-start.5 = (bf16[72,3072]{1,0:T(8,128)(2,1)S(1)}, bf16[72,3072]{1,0:T(8,128)(2,1)}, u32[]{:S(2)}) copy-start(bf16[72,3072]{1,0:T(8,128)(2,1)} %get-tuple-element.25) | copy-start | bytes 1327108
  49.8 4.1 %copy-start.6 = (bf16[72,3072]{1,0:T(8,128)(2,1)S(1)}, bf16[72,3072]{1,0:T(8,128)(2,1)}, u32[]{:S(2)}) copy-start(bf16[72,3072]{1,0:T(8,128)(2,1)} %get-tuple-element.26) | copy-start | bytes 1327108
  49.8 4.1 %copy-start.7 = (bf16[72,3072]{1,0:T(8,128)(2,1)S(1)}, bf16[72,3072]{1,0:T(8,128)(2,1)}, u32[]{:S(2)}) copy-start(bf16[72,3072]{1,0:T(8,128)(2,1)} %get-tuple-element.27) | copy-start | bytes 1327108
  49.8 4.1 %copy-start.8 = (bf16[72,3072]{1,0:T(8,128)(2,1)S(1)}, bf16[72,3072]{1,0:T(8,128)(2,1)}, u32[]{:S(2)}) copy-start(bf16[72,3072]{1,0:T(8,128)(2,1)} %get-tuple-element.28) | copy-start | bytes 1327108
  51.1 4.3 %copy-start.4 = (bf16[288,3072]{1,0:T(8,128)(2,1)}, bf16[288,3072]{1,0:T(8,128)(2,1)S(1)}, u32[]{:S(2)}) copy-start(bf16[288,3072]{1,0:T(8,128)(2,1)S(1)} %constant_dynamic-update-slice_fusion) | copy-start | bytes 5308420
  51.6 14.6 %collective-permute-start.3 = (bf16[448,384]{1,0:T(8,128)(2,1)S(1)}, bf16[448,384]{1,0:T(8,128)(2,1)S(1)}, u32[]{:S(2)}, u32[]{:S(2)}) collective-permute-start(bf16[448,384]{1,0:T(8,128)(2,1)S(1)} %convolution_convert_fusion.1), channel_id=1, source_target_pairs={{0,4},{4,8},{8,12},{12,16},{16,20},{20,24},{24,28},{28,32},{32,36}... | collective-permute-start | bytes 1032200 | tf_op jit(solution)/shard_map/ppermute | solution.py:121
  55.4 37.9 %all-to-all-start.2 = ((bf16[4,72,3072]{2,1,0:T(8,128)(2,1)}), bf16[4,72,3072]{2,1,0:T(8,128)(2,1)S(1)}, u32[]{:S(2)}, u32[]{:S(2)}) async-start(bf16[4,72,3072]{2,1,0:T(8,128)(2,1)} %pad_maximum_fusion), calls=%async_computation.2 | async-start | bytes 3538944 | tf_op jit(solution)/shard_map/all_to_all | solution.py:109
  61.9 11.6 %collective-permute-start.11 = (bf16[448,384]{1,0:T(8,128)(2,1)S(1)}, bf16[448,384]{1,0:T(8,128)(2,1)S(1)}, u32[]{:S(2)}, u32[]{:S(2)}) collective-permute-start(bf16[448,384]{1,0:T(8,128)(2,1)S(1)} %convolution_convert_fusion), channel_id=1, source_target_pairs={{0,60},{4,0},{8,4},{12,8},{16,12},{20,16},{24,20},{28,24},{32,28},... | collective-permute-start | bytes 1032200 | tf_op jit(solution)/shard_map/ppermute | solution.py:124
  67.5 12.7 %collective-permute-start.4 = (bf16[448,384]{1,0:T(8,128)(2,1)S(1)}, bf16[448,384]{1,0:T(8,128)(2,1)S(1)}, u32[]{:S(2)}, u32[]{:S(2)}) collective-permute-start(bf16[448,384]{1,0:T(8,128)(2,1)S(1)} %fusion.2), channel_id=1, source_target_pairs={{0,4},{4,8},{8,12},{12,16},{16,20},{20,24},{24,28},{28,32},{32,36}... | collective-permute-start | bytes 1032200 | tf_op jit(solution)/shard_map/ppermute | solution.py:121
  74.8 11.8 %collective-permute-start.12 = (bf16[448,384]{1,0:T(8,128)(2,1)S(1)}, bf16[448,384]{1,0:T(8,128)(2,1)S(1)}, u32[]{:S(2)}, u32[]{:S(2)}) collective-permute-start(bf16[448,384]{1,0:T(8,128)(2,1)S(1)} %fusion.5), channel_id=1, source_target_pairs={{0,60},{4,0},{8,4},{12,8},{16,12},{20,16},{24,20},{28,24},{32,28},... | collective-permute-start | bytes 1032200 | tf_op jit(solution)/shard_map/ppermute | solution.py:124
  82.3 12.3 %collective-permute-start.5 = (bf16[448,384]{1,0:T(8,128)(2,1)}, bf16[448,384]{1,0:T(8,128)(2,1)}, u32[]{:S(2)}, u32[]{:S(2)}) collective-permute-start(bf16[448,384]{1,0:T(8,128)(2,1)} %fusion.1), channel_id=1, source_target_pairs={{0,4},{4,8},{8,12},{12,16},{16,20},{20,24},{24,28},{28,32},{32,36}... | collective-permute-start | bytes 1032200 | tf_op jit(solution)/shard_map/ppermute | solution.py:121
  88.0 11.0 %collective-permute-start.13 = (bf16[448,384]{1,0:T(8,128)(2,1)S(1)}, bf16[448,384]{1,0:T(8,128)(2,1)S(1)}, u32[]{:S(2)}, u32[]{:S(2)}) collective-permute-start(bf16[448,384]{1,0:T(8,128)(2,1)S(1)} %fusion.4), channel_id=1, source_target_pairs={{0,60},{4,0},{8,4},{12,8},{16,12},{20,16},{24,20},{28,24},{32,28},... | collective-permute-start | bytes 1032200 | tf_op jit(solution)/shard_map/ppermute | solution.py:124
  93.3 25.3 %copy-start.3 = (bf16[4,72,3072]{2,1,0:T(8,128)(2,1)}, bf16[4,72,3072]{2,1,0:T(8,128)(2,1)S(1)}, u32[]{:S(2)}) copy-start(bf16[4,72,3072]{2,1,0:T(8,128)(2,1)S(1)} %all-to-all-done.2) | copy-start | bytes 5308420
  96.1 10.7 %collective-permute-start.6 = (bf16[448,384]{1,0:T(8,128)(2,1)S(1)}, bf16[448,384]{1,0:T(8,128)(2,1)S(1)}, u32[]{:S(2)}, u32[]{:S(2)}) collective-permute-start(bf16[448,384]{1,0:T(8,128)(2,1)S(1)} %fusion), channel_id=1, source_target_pairs={{0,4},{4,8},{8,12},{12,16},{16,20},{20,24},{24,28},{28,32},{32,36}... | collective-permute-start | bytes 1032200 | tf_op jit(solution)/shard_map/ppermute | solution.py:121
  100.3 10.1 %collective-permute-start.14 = (bf16[448,384]{1,0:T(8,128)(2,1)S(1)}, bf16[448,384]{1,0:T(8,128)(2,1)S(1)}, u32[]{:S(2)}, u32[]{:S(2)}) collective-permute-start(bf16[448,384]{1,0:T(8,128)(2,1)S(1)} %fusion.3), channel_id=1, source_target_pairs={{0,60},{4,0},{8,4},{12,8},{16,12},{20,16},{24,20},{28,24},{32,28},... | collective-permute-start | bytes 1032200 | tf_op jit(solution)/shard_map/ppermute | solution.py:124
  106.8 9.8 %collective-permute-start.7 = (bf16[448,384]{1,0:T(8,128)(2,1)S(1)}, bf16[448,384]{1,0:T(8,128)(2,1)S(1)}, u32[]{:S(2)}, u32[]{:S(2)}) collective-permute-start(bf16[448,384]{1,0:T(8,128)(2,1)S(1)} %add_convert_fusion.6), channel_id=1, source_target_pairs={{0,4},{4,8},{8,12},{12,16},{16,20},{20,24},{24,28},{28,32},{32,36}... | collective-permute-start | bytes 1032200 | tf_op jit(solution)/shard_map/ppermute | solution.py:121
  110.5 9.5 %collective-permute-start.15 = (bf16[448,384]{1,0:T(8,128)(2,1)S(1)}, bf16[448,384]{1,0:T(8,128)(2,1)S(1)}, u32[]{:S(2)}, u32[]{:S(2)}) collective-permute-start(bf16[448,384]{1,0:T(8,128)(2,1)S(1)} %add_convert_fusion.2), channel_id=1, source_target_pairs={{0,60},{4,0},{8,4},{12,8},{16,12},{20,16},{24,20},{28,24},{32,28},... | collective-permute-start | bytes 1032200 | tf_op jit(solution)/shard_map/ppermute | solution.py:124
  116.7 9.2 %collective-permute-start.8 = (bf16[448,384]{1,0:T(8,128)(2,1)S(1)}, bf16[448,384]{1,0:T(8,128)(2,1)S(1)}, u32[]{:S(2)}, u32[]{:S(2)}) collective-permute-start(bf16[448,384]{1,0:T(8,128)(2,1)S(1)} %add_convert_fusion.5), channel_id=1, source_target_pairs={{0,4},{4,8},{8,12},{12,16},{16,20},{20,24},{24,28},{28,32},{32,36}... | collective-permute-start | bytes 1032200 | tf_op jit(solution)/shard_map/ppermute | solution.py:121
  119.1 9.1 %copy-start.2 = (bf16[288,448]{1,0:T(8,128)(2,1)S(1)}, bf16[288,448]{1,0:T(8,128)(2,1)}, u32[]{:S(2)}) copy-start(bf16[288,448]{1,0:T(8,128)(2,1)} %copy-done.1) | copy-start | bytes 774148
  120.0 9.5 %collective-permute-start.16 = (bf16[448,384]{1,0:T(8,128)(2,1)S(1)}, bf16[448,384]{1,0:T(8,128)(2,1)S(1)}, u32[]{:S(2)}, u32[]{:S(2)}) collective-permute-start(bf16[448,384]{1,0:T(8,128)(2,1)S(1)} %add_convert_fusion.1), channel_id=1, source_target_pairs={{0,60},{4,0},{8,4},{12,8},{16,12},{20,16},{24,20},{28,24},{32,28},... | collective-permute-start | bytes 1032200 | tf_op jit(solution)/shard_map/ppermute | solution.py:124
  126.0 12.2 %copy-start.10 = (s32[448]{0:T(512)S(1)}, s32[448]{0:T(512)}, u32[]{:S(2)}) copy-start(s32[448]{0:T(512)} %param.8) | copy-start | bytes 5380
  126.0 12.2 %copy-start = (bf16[72,24576]{1,0:T(8,128)(2,1)S(1)}, bf16[72,24576]{1,0:T(8,128)(2,1)}, u32[]{:S(2)}) copy-start(bf16[72,24576]{1,0:T(8,128)(2,1)} %table_ref.2) | copy-start | bytes 10616836
  126.0 9.5 %collective-permute-start.9 = (bf16[448,384]{1,0:T(8,128)(2,1)S(1)}, bf16[448,384]{1,0:T(8,128)(2,1)S(1)}, u32[]{:S(2)}, u32[]{:S(2)}) collective-permute-start(bf16[448,384]{1,0:T(8,128)(2,1)S(1)} %add_convert_fusion.4), channel_id=1, source_target_pairs={{0,4},{4,8},{8,12},{12,16},{16,20},{20,24},{24,28},{28,32},{32,36}... | collective-permute-start | bytes 1032200 | tf_op jit(solution)/shard_map/ppermute | solution.py:121
  130.4 18.0 %collective-permute-start.17 = (bf16[448,384]{1,0:T(8,128)(2,1)}, bf16[448,384]{1,0:T(8,128)(2,1)}, u32[]{:S(2)}, u32[]{:S(2)}) collective-permute-start(bf16[448,384]{1,0:T(8,128)(2,1)} %add_convert_fusion), channel_id=1, source_target_pairs={{0,60},{4,0},{8,4},{12,8},{16,12},{20,16},{24,20},{28,24},{32,28},... | collective-permute-start | bytes 1032200 | tf_op jit(solution)/shard_map/ppermute | solution.py:124
  136.3 12.1 %collective-permute-start.10 = (bf16[448,384]{1,0:T(8,128)(2,1)}, bf16[448,384]{1,0:T(8,128)(2,1)}, u32[]{:S(2)}, u32[]{:S(2)}) collective-permute-start(bf16[448,384]{1,0:T(8,128)(2,1)} %add_convert_fusion.3), channel_id=1, source_target_pairs={{0,4},{4,8},{8,12},{12,16},{16,20},{20,24},{24,28},{28,32},{32,36}... | collective-permute-start | bytes 1032200 | tf_op jit(solution)/shard_map/ppermute | solution.py:121
  151.1 20.7 %all-to-all-start.3 = ((f32[32,8,128]{2,1,0:T(8,128)}), f32[32,8,128]{2,1,0:T(8,128)S(1)}, u32[]{:S(2)}, u32[]{:S(2)}) async-start(f32[32,8,128]{2,1,0:T(8,128)} %broadcast_in_dim.81), calls=%async_computation.3 | async-start | bytes 262144 | tf_op jit(solution)/shard_map/all_to_all | solution.py:21
  172.6 14.6 %all-to-all-start = ((bf16[8,72,448]{2,1,0:T(8,128)(2,1)}), bf16[8,72,448]{2,1,0:T(8,128)(2,1)S(1)}, u32[]{:S(2)}, u32[]{:S(2)}) async-start(bf16[8,72,448]{2,1,0:T(8,128)(2,1)} %broadcast_in_dim.76), calls=%async_computation | async-start | bytes 1179648 | tf_op jit(solution)/shard_map/all_to_all | solution.py:21
  187.9 16.2 %all-to-all-start.4 = ((f32[16,8,128]{2,1,0:T(8,128)}), f32[16,8,128]{2,1,0:T(8,128)S(1)}, u32[]{:S(2)}, u32[]{:S(2)}) async-start(f32[16,8,128]{2,1,0:T(8,128)} %broadcast_in_dim.82), calls=%async_computation.4 | async-start | bytes 131072 | tf_op jit(solution)/shard_map/all_to_all | solution.py:21

commit v2 on v1

--- a/solution.py
+++ b/solution.py
@@ -25,21 +25,25 @@
     return jnp.pad(x, (0, LANES - x.shape[0])).reshape(LANES // 128, 128)
 
 
-def arrange(table, places, near_index, near_n):
+def arrange(table, places, near_index, near_n, joined):
     share, span_cols = table.shape
-    slots = places.shape[0]
-    cols = span_cols // (lax.axis_size(FAR) * near_n)
+    cores, slots = places.shape
+    per = span_cols // (lax.axis_size(FAR) * near_n)
+    cols = per * cores
 
     def kernel(places_ref, near_ref, table_ref, *refs):
-        out_refs, sems = refs[:near_n], refs[near_n]
+        sems = refs[-1]
         copies = []
         for k in range(near_n):
+            out_ref = refs[0].at[k] if joined else refs[k]
+            near = near_ref[0] ^ k
+            core = near % cores
             for j in range(slots):
-                block = places_ref[j] * near_n + (near_ref[0] ^ k)
+                block = places_ref[core * slots + j] * near_n + near - core
                 copies.append(
                     pltpu.make_async_copy(
-                        table_ref.at[:, pl.ds(pl.multiple_of(block * cols, cols), cols)],
-                        out_refs[k].at[:, pl.ds(j * cols, cols)],
+                        table_ref.at[:, pl.ds(pl.multiple_of(block * per, per), cols)],
+                        out_ref.at[:, pl.ds(j * cols, cols)],
                         sems.at[k * slots + j],
                     )
                 )
@@ -52,17 +56,12 @@
     return pl.pallas_call(
         kernel,
         in_specs=[smem, smem, pl.BlockSpec(memory_space=pltpu.HBM)],
-        out_specs=[vmem] * near_n,
-        out_shape=[jax.ShapeDtypeStruct((share, slots * cols), table.dtype)] * near_n,
+        out_specs=[vmem] * (1 if joined else near_n),
+        out_shape=[jax.ShapeDtypeStruct((near_n, share, slots * cols), table.dtype)]
+        if joined
+        else [jax.ShapeDtypeStruct((share, slots * cols), table.dtype)] * near_n,
         scratch_shapes=[pltpu.SemaphoreType.DMA((near_n * slots,))],
-    )(places, near_index[None], table)
-
-
-def add_partial(x, w, slot, cols, received, dtype):
-    y = jnp.dot(x, w[:, slot * cols : (slot + 1) * cols], preferred_element_type=jnp.float32)
-    for r in received:
-        y = y + r.astype(jnp.float32)
-    return y.astype(dtype)
+    )(places.reshape(-1), near_index[None], table)
 
 
 def layer(table, hidden, gain, ids):
@@ -76,16 +75,16 @@
     depth = lax.axis_index(FAR)
     steps = far_n // 2
 
-    order = []
-    for s in range(steps):
-        order += [steps - s, (s - steps + 1)]
-    places = (depth + jnp.array(order, jnp.int32)) % far_n
-    early = far_n // 2
+    core = lax.axis_index("core")
+    cores = lax.axis_size("core")
+    offsets = [[steps - j for j in range(steps)], [j - steps + 1 for j in range(steps)]]
+    places = (depth + jnp.array(offsets, jnp.int32)) % far_n
+    early = steps // 2
 
     fill = jnp.broadcast_to(gain[:, None], (share, LANES - tok))
     both = jnp.concatenate([hidden.T, fill], axis=1)
     near_index = lax.axis_index(NEAR)
-    first = arrange(table, places[:early], near_index, near_n)
+    first = arrange(table, places[:, :early], near_index, near_n, False)
     both = lax.all_gather(both, NEAR, axis=0, tiled=True)
     first, both = lax.optimization_barrier((first, both))
     swapped = jnp.zeros((near_n * share, first[0].shape[1]), table.dtype)
@@ -104,25 +103,33 @@
     mean_sq = squares.sum(axis=0).reshape(LANES)[:tok] / width
     normed = (states * gains * lax.rsqrt(mean_sq + 1e-06)[None, :]).astype(jnp.bfloat16).T
 
-    second = arrange(late_table, places[early:], near_index * 0, near_n)
-    second = jnp.stack(second)
+    (second,) = arrange(late_table, places[:, early:], near_index * 0, near_n, True)
     second = lax.all_to_all(second, NEAR, split_axis=0, concat_axis=0, tiled=True)
     second = second.reshape(near_n * share, -1)
 
-    def part(slot, received, dtype=jnp.bfloat16):
-        w, at = (first, slot) if slot < early else (second, slot - early)
-        return add_partial(normed, w, at, voc_cols, received, dtype)
+    def onward(j):
+        up = [(2 * i, 2 * ((i + 1) % far_n)) for i in range(far_n)]
+        down = [(2 * i + 1, 2 * ((i - 1) % far_n) + 1) for i in range(far_n)]
+        return up + down if j < steps - 1 else up
 
-    ahead = [(i, (i + 1) % far_n) for i in range(far_n)]
-    behind = [(i, (i - 1) % far_n) for i in range(far_n)]
-    up, down = [], []
-    for s in range(steps):
-        out = part(2 * s, up)
-        up = [lax.ppermute(out, FAR, ahead)]
-        if s < steps - 1:
-            out = part(2 * s + 1, down)
-            down = [lax.ppermute(out, FAR, behind)]
-    logits = part(2 * steps - 1, up + down, jnp.float32)
+    pair_cols = cores * voc_cols
+    streams = 2
+    rows = tok // streams
+    came, out = [None] * streams, [None] * streams
+    for j in range(steps):
+        w, at = (first, j) if j < early else (second, j - early)
+        w = w[:, at * pair_cols : (at + 1) * pair_cols]
+        for h in range(streams):
+            y = jnp.dot(normed[h * rows : (h + 1) * rows], w, preferred_element_type=jnp.float32)
+            if j:
+                y = y + came[h].astype(jnp.float32)
+            out[h] = y.astype(jnp.bfloat16)
+            came[h] = lax.ppermute(out[h], (FAR, "core"), onward(j))
+    arms = jnp.concatenate([jnp.where(core == 0, c, o) for c, o in zip(came, out)])
+    kept = lax.dynamic_slice_in_dim(arms, core * voc_cols, voc_cols, axis=1)
+    given = lax.dynamic_slice_in_dim(arms, (1 - core) * voc_cols, voc_cols, axis=1)
+    given = lax.ppermute(given, "core", [(0, 1), (1, 0)])
+    logits = kept.astype(jnp.float32) + given.astype(jnp.float32)
 
     local_ids = ids - group_index * span_cols
     inside = jnp.logical_and(local_ids >= 0, local_ids < span_cols)

time: 209 us -> 217 us (1.038)
  starting transfers between devices: 95.1 us -> 112 us
  matrix products: 16.4 us -> 8.84 us
  waiting for transfers between devices: 48.3 us -> 43.9 us
  other arithmetic: 9.03 us -> 12 us
    ppermute x15 -> x17, starting transfers between devices: 51.3 us -> 75.3 us  [the longest x16 56.5 us: layer(): came[h] = lax.ppermute(out[h], (FAR, 'core'), onward(j))]
    ppermute x15 -> x17, waiting for transfers between devices: 12.5 us -> 4.44 us  [the longest x16 4.44 us: layer(): came[h] = lax.ppermute(out[h], (FAR, 'core'), onward(j))]
    dot_general x16, matrix products: 16.4 us -> 8.84 us  [layer(): jnp.dot(normed[h * rows:(h + 1) * rows], w, preferred_element_type=jnp.fl...]
    all_to_all x4, starting transfers between devices: 30.9 us -> 24.3 us  [copies_of(): return lax.all_to_all(many, axes, split_axis=0, concat_axis=0, tiled=True)]
    all_to_all x4, waiting for transfers between devices: 35.8 us -> 39.4 us  [copies_of(): return lax.all_to_all(many, axes, split_axis=0, concat_axis=0, tiled=True)]
    select_n x1 -> x3, other arithmetic: 0.67 us -> 2.85 us  [the longest x2 2.16 us: layer(): jnp.where(core == 0, c, o)]
  transfers between devices with their start and end apart: 23 -> 25, of which waited for: 13 -> 12; matrix products, arithmetic and copies ran while one was open for 15% -> 12% of each run, Pallas kernels for 2% -> 2%
where the time goes in v2:
time: 217 us; the launch traced here: 215 us
  starting transfers between devices  112 us (52%)
  waiting for transfers between devices  43.9 us (20%)
  local copies, waits for them, and re-layouts  17.4 us (8%)
  blocking collectives  12.5 us (6%)
  other arithmetic  12 us (6%)
  matrix products  8.84 us (4%)
  Pallas kernels  7.07 us (3%)
    ppermute x16, starting transfers between devices, layer(): came[h] = lax.ppermute(out[h], (FAR, 'core'), onward(j))  56.5 us
    all_to_all x4, waiting for transfers between devices, copies_of(): return lax.all_to_all(many, axes, split_axis=0, concat_axis=0, tiled=True)  39.4 us
    all_to_all x4, starting transfers between devices, copies_of(): return lax.all_to_all(many, axes, split_axis=0, concat_axis=0, tiled=True)  24.3 us
    ppermute x1, starting transfers between devices, layer(): given = lax.ppermute(given, 'core', [(0, 1), (1, 0)])  18.9 us
    all_gather x1, blocking collectives, layer(): both = lax.all_gather(both, NEAR, axis=0, tiled=True)  12.5 us
    dot_general x16, matrix products, layer(): jnp.dot(normed[h * rows:(h + 1) * rows], w, preferred_element_type=jnp.fl...  8.84 us
    ppermute x3, starting transfers between devices, layer(): slab = lax.ppermute(slab, NEAR, [(i, i ^ k) for i in range(near_n)])  7.87 us
    pallas_call x2, Pallas kernels, arrange(): pl.pallas_call(kernel, in_specs=[smem, smem, pl.BlockSpec(memory_space=pl...  7.07 us
  transfers between devices with their start and end apart: 25, of which 12 were waited for; matrix products, arithmetic and copies ran while one was open for 12% of the time, Pallas kernels for 2%

profile of v2, /device:TPU:1, one launch (start us, length us, event | category | flops | bytes accessed | tf_op | source)
XLA Modules:
  0.0 215.3 jit_solution(16164125181044119590)
XLA Ops:
  0.6 0.7 and_select_fusion
  1.4 0.6 reshape.77.places_ref
  2.0 0.7 broadcast_in_dim.72
  2.7 1.0 pad_maximum_fusion
  3.7 12.5 %all_gather.3 = bf16[288,512]{1,0:T(8,128)(2,1)S(1)} all-gather(bf16[72,512]{1,0:T(8,128)(2,1)S(1)} %pad_maximum_fusion), channel_id=1, replica_groups=mesh['group_0'=4,'group_1'=2,'depth'=16,'row'=2,'core'=2] {'row','core'}, dimensions={0}, use_global_device_ids=true | all-gather | bytes 368640 | tf_op jit(solution)/shard_map/all_gather | solution.py:88
  16.2 3.5 %shard_map.76 = (bf16[72,3072]{1,0:T(8,128)(2,1)}, bf16[72,3072]{1,0:T(8,128)(2,1)}, bf16[72,3072]{1,0:T(8,128)(2,1)}, bf16[72,3072]{1,0:T(8,128)(2,1)}) custom-call(s32[8]{0:T(128)} %reshape.77.places_ref, s32[1]{0:T(128)} %bitcast.near_ref, bf16[72,24576]{1,0:T(8,128)(2,1)} %table_ref.2), custom_call_target="tpu_custom_call" | custom-call | tf_op jit(solution)/shard_map/pallas_call | solution.py:56
  19.8 2.1 collective-permute-start
  21.8 2.2 %collective-permute-start.1 = (bf16[72,3072]{1,0:T(8,128)(2,1)}, bf16[72,3072]{1,0:T(8,128)(2,1)S(1)}, u32[]{:S(2)}, u32[]{:S(2)}) collective-permute-start(bf16[72,3072]{1,0:T(8,128)(2,1)} %get-tuple-element.23), channel_id=1, source_target_pairs={{0,2},{1,3},{2,0},{3,1},{4,6},{5,7},{6,4},{7,5},{8,10},{9,11},{10,... | collective-permute-start | bytes 1327112 | tf_op jit(solution)/shard_map/ppermute | solution.py:94
  24.1 3.6 %collective-permute-start.2 = (bf16[72,3072]{1,0:T(8,128)(2,1)}, bf16[72,3072]{1,0:T(8,128)(2,1)S(1)}, u32[]{:S(2)}, u32[]{:S(2)}) collective-permute-start(bf16[72,3072]{1,0:T(8,128)(2,1)} %get-tuple-element.24), channel_id=1, source_target_pairs={{0,3},{1,2},{2,1},{3,0},{4,7},{5,6},{6,5},{7,4},{8,11},{9,10},{10,... | collective-permute-start | bytes 1327112 | tf_op jit(solution)/shard_map/ppermute | solution.py:94
  27.8 0.6 broadcast_in_dim.78
  28.4 9.7 %all-to-all-start.1 = ((f32[16,4,128]{2,1,0:T(4,128)}), f32[16,4,128]{2,1,0:T(4,128)S(1)}, u32[]{:S(2)}, u32[]{:S(2)}) async-start(f32[16,4,128]{2,1,0:T(4,128)} %broadcast_in_dim.78), calls=%async_computation.1 | async-start | bytes 65536 | tf_op jit(solution)/shard_map/all_to_all | solution.py:21
  38.4 0.8 copy-done.6
  39.4 10.2 %all-to-all-done.1 = f32[16,4,128]{2,1,0:T(4,128)S(1)} async-done(((f32[16,4,128]{2,1,0:T(4,128)}), f32[16,4,128]{2,1,0:T(4,128)S(1)}, u32[]{:S(2)}, u32[]{:S(2)}) %all-to-all-start.1) | async-done | bytes 32800 | tf_op jit(solution)/shard_map/all_to_all | solution.py:21
  49.8 1.1 constant_dynamic-update-slice_fusion.2
  51.0 0.5 convolution_convert_fusion
  51.5 2.8 %collective-permute-start.11 = (bf16[224,768]{1,0:T(8,128)(2,1)S(1)}, bf16[224,768]{1,0:T(8,128)(2,1)S(1)}, u32[]{:S(2)}, u32[]{:S(2)}) collective-permute-start(bf16[224,768]{1,0:T(8,128)(2,1)S(1)} %convolution_convert_fusion), channel_id=1, source_target_pairs={{0,4},{4,8},{8,12},{12,16},{16,20},{20,24},{24,28},{28,32},{32,36}... | collective-permute-start | bytes 1032200 | tf_op jit(solution)/shard_map/ppermute | solution.py:127
  54.2 0.6 reshape.79.places_ref
  54.8 3.6 %shard_map.77 = bf16[4,72,3072]{2,1,0:T(8,128)(2,1)} custom-call(s32[8]{0:T(128)} %reshape.79.places_ref, s32[1]{0:T(128)} %constant.84.clone.1.near_ref, bf16[72,24576]{1,0:T(8,128)(2,1)} %table_ref.2), custom_call_target="tpu_custom_call" | custom-call | tf_op jit(solution)/shard_map/pallas_call | solution.py:56
  58.4 4.8 %all-to-all-start.2 = ((bf16[4,72,3072]{2,1,0:T(8,128)(2,1)}), bf16[4,72,3072]{2,1,0:T(8,128)(2,1)S(1)}, u32[]{:S(2)}, u32[]{:S(2)}) async-start(bf16[4,72,3072]{2,1,0:T(8,128)(2,1)} %shard_map.77), calls=%async_computation.2 | async-start | bytes 3538944 | tf_op jit(solution)/shard_map/all_to_all | solution.py:107
  63.1 1.5 convolution_convert_fusion.1
  64.6 4.2 %collective-permute-start.3 = (bf16[224,768]{1,0:T(8,128)(2,1)S(1)}, bf16[224,768]{1,0:T(8,128)(2,1)S(1)}, u32[]{:S(2)}, u32[]{:S(2)}) collective-permute-start(bf16[224,768]{1,0:T(8,128)(2,1)S(1)} %convolution_convert_fusion.1), channel_id=1, source_target_pairs={{0,4},{4,8},{8,12},{12,16},{16,20},{20,24},{24,28},{28,32},{32,36}... | collective-permute-start | bytes 1032200 | tf_op jit(solution)/shard_map/ppermute | solution.py:127
  68.9 1.5 fusion.5
  70.4 1.9 collective-permute-start.12
  72.3 0.7 collective-permute-done.3
  73.4 5.0 %collective-permute-start.4 = (bf16[224,768]{1,0:T(8,128)(2,1)S(1)}, bf16[224,768]{1,0:T(8,128)(2,1)S(1)}, u32[]{:S(2)}, u32[]{:S(2)}) collective-permute-start(bf16[224,768]{1,0:T(8,128)(2,1)S(1)} %fusion.2), channel_id=1, source_target_pairs={{0,4},{4,8},{8,12},{12,16},{16,20},{20,24},{24,28},{28,32},{32,36}... | collective-permute-start | bytes 1032200 | tf_op jit(solution)/shard_map/ppermute | solution.py:127
  78.7 0.5 fusion.4
  79.2 3.1 %collective-permute-start.13 = (bf16[224,768]{1,0:T(8,128)(2,1)S(1)}, bf16[224,768]{1,0:T(8,128)(2,1)S(1)}, u32[]{:S(2)}, u32[]{:S(2)}) collective-permute-start(bf16[224,768]{1,0:T(8,128)(2,1)S(1)} %fusion.4), channel_id=1, source_target_pairs={{0,4},{4,8},{8,12},{12,16},{16,20},{20,24},{24,28},{28,32},{32,36}... | collective-permute-start | bytes 1032200 | tf_op jit(solution)/shard_map/ppermute | solution.py:127
  83.0 5.0 %collective-permute-start.5 = (bf16[224,768]{1,0:T(8,128)(2,1)S(1)}, bf16[224,768]{1,0:T(8,128)(2,1)S(1)}, u32[]{:S(2)}, u32[]{:S(2)}) collective-permute-start(bf16[224,768]{1,0:T(8,128)(2,1)S(1)} %fusion.1), channel_id=1, source_target_pairs={{0,4},{4,8},{8,12},{12,16},{16,20},{20,24},{24,28},{28,32},{32,36}... | collective-permute-start | bytes 1032200 | tf_op jit(solution)/shard_map/ppermute | solution.py:127
  88.1 0.5 fusion.14
  90.0 0.5 fusion.3
  90.5 1.9 collective-permute-start.14
  92.8 4.8 %collective-permute-start.6 = (bf16[224,768]{1,0:T(8,128)(2,1)S(1)}, bf16[224,768]{1,0:T(8,128)(2,1)S(1)}, u32[]{:S(2)}, u32[]{:S(2)}) collective-permute-start(bf16[224,768]{1,0:T(8,128)(2,1)S(1)} %fusion), channel_id=1, source_target_pairs={{0,4},{4,8},{8,12},{12,16},{16,20},{20,24},{24,28},{28,32},{32,36}... | collective-permute-start | bytes 1032200 | tf_op jit(solution)/shard_map/ppermute | solution.py:127
  98.0 0.8 collective-permute-done.14
  98.8 2.8 %collective-permute-start.15 = (bf16[224,768]{1,0:T(8,128)(2,1)S(1)}, bf16[224,768]{1,0:T(8,128)(2,1)S(1)}, u32[]{:S(2)}, u32[]{:S(2)}) collective-permute-start(bf16[224,768]{1,0:T(8,128)(2,1)S(1)} %add_convert_fusion.3), channel_id=1, source_target_pairs={{0,4},{4,8},{8,12},{12,16},{16,20},{20,24},{24,28},{28,32},{32,36}... | collective-permute-start | bytes 1032200 | tf_op jit(solution)/shard_map/ppermute | solution.py:127
  101.7 0.5 collective-permute-done.6
  102.2 4.7 %collective-permute-start.7 = (bf16[224,768]{1,0:T(8,128)(2,1)S(1)}, bf16[224,768]{1,0:T(8,128)(2,1)S(1)}, u32[]{:S(2)}, u32[]{:S(2)}) collective-permute-start(bf16[224,768]{1,0:T(8,128)(2,1)S(1)} %add_convert_fusion.7), channel_id=1, source_target_pairs={{0,4},{4,8},{8,12},{12,16},{16,20},{20,24},{24,28},{28,32},{32,36}... | collective-permute-start | bytes 1032200 | tf_op jit(solution)/shard_map/ppermute | solution.py:127
  107.3 3.6 %collective-permute-start.16 = (bf16[224,768]{1,0:T(8,128)(2,1)S(1)}, bf16[224,768]{1,0:T(8,128)(2,1)S(1)}, u32[]{:S(2)}, u32[]{:S(2)}) collective-permute-start(bf16[224,768]{1,0:T(8,128)(2,1)S(1)} %add_convert_fusion.2), channel_id=1, source_target_pairs={{0,4},{4,8},{8,12},{12,16},{16,20},{20,24},{24,28},{28,32},{32,36}... | collective-permute-start | bytes 1032200 | tf_op jit(solution)/shard_map/ppermute | solution.py:127
  111.1 5.0 %collective-permute-start.8 = (bf16[224,768]{1,0:T(8,128)(2,1)S(1)}, bf16[224,768]{1,0:T(8,128)(2,1)S(1)}, u32[]{:S(2)}, u32[]{:S(2)}) collective-permute-start(bf16[224,768]{1,0:T(8,128)(2,1)S(1)} %add_convert_fusion.6), channel_id=1, source_target_pairs={{0,4},{4,8},{8,12},{12,16},{16,20},{20,24},{24,28},{28,32},{32,36}... | collective-permute-start | bytes 1032200 | tf_op jit(solution)/shard_map/ppermute | solution.py:127
  116.6 3.6 %collective-permute-start.17 = (bf16[224,768]{1,0:T(8,128)(2,1)S(1)}, bf16[224,768]{1,0:T(8,128)(2,1)S(1)}, u32[]{:S(2)}, u32[]{:S(2)}) collective-permute-start(bf16[224,768]{1,0:T(8,128)(2,1)S(1)} %add_convert_fusion.1), channel_id=1, source_target_pairs={{0,4},{4,8},{8,12},{12,16},{16,20},{20,24},{24,28},{28,32},{32,36}... | collective-permute-start | bytes 1032200 | tf_op jit(solution)/shard_map/ppermute | solution.py:127
  120.4 5.0 %collective-permute-start.9 = (bf16[224,768]{1,0:T(8,128)(2,1)S(1)}, bf16[224,768]{1,0:T(8,128)(2,1)S(1)}, u32[]{:S(2)}, u32[]{:S(2)}) collective-permute-start(bf16[224,768]{1,0:T(8,128)(2,1)S(1)} %add_convert_fusion.5), channel_id=1, source_target_pairs={{0,4},{4,8},{8,12},{12,16},{16,20},{20,24},{24,28},{28,32},{32,36}... | collective-permute-start | bytes 1032200 | tf_op jit(solution)/shard_map/ppermute | solution.py:127
  125.8 0.8 add_convert_fusion
  126.6 1.4 collective-permute-start.18
  128.0 1.6 collective-permute-done.9
  129.6 0.8 add_convert_fusion.4
  130.4 1.5 collective-permute-start.10
  131.9 1.0 broadcast_select_fusion
  133.0 1.1 broadcast_select_fusion.1
  134.1 0.8 fusion.31
  135.0 18.9 %collective-permute-start.19 = (bf16[448,384]{1,0:T(8,128)(2,1)}, bf16[448,384]{1,0:T(8,128)(2,1)}, u32[]{:S(2)}, u32[]{:S(2)}) collective-permute-start(bf16[448,384]{1,0:T(8,128)(2,1)} %fusion.31), channel_id=1, source_target_pairs={{0,1},{1,0},{2,3},{3,2},{4,5},{5,4},{6,7},{7,6},{8,9},{9,8},{10,11... | collective-permute-start | bytes 1032200 | tf_op jit(solution)/shard_map/ppermute | solution.py:131
  153.9 5.2 %copy.14 = bf16[72,24576]{0,1:T(8,128)(2,1)} copy(bf16[72,24576]{1,0:T(8,128)(2,1)S(1)} %copy-done) | data formatting | bytes 7077888 | tf_op jit(solution)/shard_map/optimization_barrier | solution.py:101
  159.1 4.8 %gather_fusion = bf16[448,72]{1,0:T(8,128)(2,1)S(1)} fusion(bf16[72,24576]{0,1:T(8,128)(2,1)} %copy.14, s32[1024]{0:T(1024)S(1)} %pad_clamp_fusion), kind=kCustom, calls=%fused_computation | custom fusion | bytes 130816 | tf_op jit(solution)/shard_map/jit(_take)/gather | solution.py:136
  164.0 1.5 exponential_reduce_fusion
  165.5 0.7 broadcast_in_dim.81
  166.2 7.6 %all-to-all-start.3 = ((f32[32,8,128]{2,1,0:T(8,128)}), f32[32,8,128]{2,1,0:T(8,128)S(1)}, u32[]{:S(2)}, u32[]{:S(2)}) async-start(f32[32,8,128]{2,1,0:T(8,128)} %broadcast_in_dim.81), calls=%async_computation.3 | async-start | bytes 262144 | tf_op jit(solution)/shard_map/all_to_all | solution.py:21
  174.1 7.4 %all-to-all-done.3 = f32[32,8,128]{2,1,0:T(8,128)S(1)} async-done(((f32[32,8,128]{2,1,0:T(8,128)}), f32[32,8,128]{2,1,0:T(8,128)S(1)}, u32[]{:S(2)}, u32[]{:S(2)}) %all-to-all-start.3) | async-done | bytes 131104 | tf_op jit(solution)/shard_map/all_to_all | solution.py:21
  181.5 0.9 broadcast_in_dim.76
  182.3 3.5 %all-to-all-start = ((bf16[8,72,448]{2,1,0:T(8,128)(2,1)}), bf16[8,72,448]{2,1,0:T(8,128)(2,1)S(1)}, u32[]{:S(2)}, u32[]{:S(2)}) async-start(bf16[8,72,448]{2,1,0:T(8,128)(2,1)} %broadcast_in_dim.76), calls=%async_computation | async-start | bytes 1179648 | tf_op jit(solution)/shard_map/all_to_all | solution.py:21
  185.9 11.0 %all-to-all-done = bf16[8,72,448]{2,1,0:T(8,128)(2,1)S(1)} async-done(((bf16[8,72,448]{2,1,0:T(8,128)(2,1)}), bf16[8,72,448]{2,1,0:T(8,128)(2,1)S(1)}, u32[]{:S(2)}, u32[]{:S(2)}) %all-to-all-start) | async-done | bytes 516128 | tf_op jit(solution)/shard_map/all_to_all | solution.py:21
  196.9 0.6 broadcast_in_dim.82
  197.5 3.5 %all-to-all-start.4 = ((f32[16,8,128]{2,1,0:T(8,128)}), f32[16,8,128]{2,1,0:T(8,128)S(1)}, u32[]{:S(2)}, u32[]{:S(2)}) async-start(f32[16,8,128]{2,1,0:T(8,128)} %broadcast_in_dim.82), calls=%async_computation.4 | async-start | bytes 131072 | tf_op jit(solution)/shard_map/all_to_all | solution.py:21
  201.1 0.6 fusion.34
  201.8 10.9 %all-to-all-done.4 = f32[16,8,128]{2,1,0:T(8,128)S(1)} async-done(((f32[16,8,128]{2,1,0:T(8,128)}), f32[16,8,128]{2,1,0:T(8,128)S(1)}, u32[]{:S(2)}, u32[]{:S(2)}) %all-to-all-start.4) | async-done | bytes 65568 | tf_op jit(solution)/shard_map/all_to_all | solution.py:21
  212.7 0.6 sub.33
  213.3 2.0 fusion.30
  (72 shorter events, 6.6 us)
Async XLA Ops:
  19.8 30.0 %collective-permute-start = (bf16[72,3072]{1,0:T(8,128)(2,1)}, bf16[72,3072]{1,0:T(8,128)(2,1)}, u32[]{:S(2)}, u32[]{:S(2)}) collective-permute-start(bf16[72,3072]{1,0:T(8,128)(2,1)} %get-tuple-element.22), channel_id=1, source_target_pairs={{0,1},{1,0},{2,3},{3,2},{4,5},{5,4},{6,7},{7,6},{8,9},{9,8},{10,11... | collective-permute-start | bytes 1327112 | tf_op jit(solution)/shard_map/ppermute | solution.py:94
  21.8 29.0 %collective-permute-start.1 = (bf16[72,3072]{1,0:T(8,128)(2,1)}, bf16[72,3072]{1,0:T(8,128)(2,1)S(1)}, u32[]{:S(2)}, u32[]{:S(2)}) collective-permute-start(bf16[72,3072]{1,0:T(8,128)(2,1)} %get-tuple-element.23), channel_id=1, source_target_pairs={{0,2},{1,3},{2,0},{3,1},{4,6},{5,7},{6,4},{7,5},{8,10},{9,11},{10,... | collective-permute-start | bytes 1327112 | tf_op jit(solution)/shard_map/ppermute | solution.py:94
  24.1 26.9 %collective-permute-start.2 = (bf16[72,3072]{1,0:T(8,128)(2,1)}, bf16[72,3072]{1,0:T(8,128)(2,1)S(1)}, u32[]{:S(2)}, u32[]{:S(2)}) collective-permute-start(bf16[72,3072]{1,0:T(8,128)(2,1)} %get-tuple-element.24), channel_id=1, source_target_pairs={{0,3},{1,2},{2,1},{3,0},{4,7},{5,6},{6,5},{7,4},{8,11},{9,10},{10,... | collective-permute-start | bytes 1327112 | tf_op jit(solution)/shard_map/ppermute | solution.py:94
  28.4 21.2 %all-to-all-start.1 = ((f32[16,4,128]{2,1,0:T(4,128)}), f32[16,4,128]{2,1,0:T(4,128)S(1)}, u32[]{:S(2)}, u32[]{:S(2)}) async-start(f32[16,4,128]{2,1,0:T(4,128)} %broadcast_in_dim.78), calls=%async_computation.1 | async-start | bytes 65536 | tf_op jit(solution)/shard_map/all_to_all | solution.py:21
  38.1 1.0 copy-start.6
  51.0 7.4 %copy-start.3 = (bf16[288,3072]{1,0:T(8,128)(2,1)}, bf16[288,3072]{1,0:T(8,128)(2,1)S(1)}, u32[]{:S(2)}) copy-start(bf16[288,3072]{1,0:T(8,128)(2,1)S(1)} %constant_dynamic-update-slice_fusion) | copy-start | bytes 5308420
  51.5 17.4 %collective-permute-start.11 = (bf16[224,768]{1,0:T(8,128)(2,1)S(1)}, bf16[224,768]{1,0:T(8,128)(2,1)S(1)}, u32[]{:S(2)}, u32[]{:S(2)}) collective-permute-start(bf16[224,768]{1,0:T(8,128)(2,1)S(1)} %convolution_convert_fusion), channel_id=1, source_target_pairs={{0,4},{4,8},{8,12},{12,16},{16,20},{20,24},{24,28},{28,32},{32,36}... | collective-permute-start | bytes 1032200 | tf_op jit(solution)/shard_map/ppermute | solution.py:127
  58.4 29.7 %all-to-all-start.2 = ((bf16[4,72,3072]{2,1,0:T(8,128)(2,1)}), bf16[4,72,3072]{2,1,0:T(8,128)(2,1)S(1)}, u32[]{:S(2)}, u32[]{:S(2)}) async-start(bf16[4,72,3072]{2,1,0:T(8,128)(2,1)} %shard_map.77), calls=%async_computation.2 | async-start | bytes 3538944 | tf_op jit(solution)/shard_map/all_to_all | solution.py:107
  63.1 9.9 %copy-start.4 = (bf16[288,3072]{1,0:T(8,128)(2,1)S(1)}, bf16[288,3072]{1,0:T(8,128)(2,1)}, u32[]{:S(2)}) copy-start(bf16[288,3072]{1,0:T(8,128)(2,1)} %copy-done.3) | copy-start | bytes 5308420
  64.6 8.4 %collective-permute-start.3 = (bf16[224,768]{1,0:T(8,128)(2,1)S(1)}, bf16[224,768]{1,0:T(8,128)(2,1)S(1)}, u32[]{:S(2)}, u32[]{:S(2)}) collective-permute-start(bf16[224,768]{1,0:T(8,128)(2,1)S(1)} %convolution_convert_fusion.1), channel_id=1, source_target_pairs={{0,4},{4,8},{8,12},{12,16},{16,20},{20,24},{24,28},{28,32},{32,36}... | collective-permute-start | bytes 1032200 | tf_op jit(solution)/shard_map/ppermute | solution.py:127
  70.4 8.3 %collective-permute-start.12 = (bf16[224,768]{1,0:T(8,128)(2,1)S(1)}, bf16[224,768]{1,0:T(8,128)(2,1)S(1)}, u32[]{:S(2)}, u32[]{:S(2)}) collective-permute-start(bf16[224,768]{1,0:T(8,128)(2,1)S(1)} %fusion.5), channel_id=1, source_target_pairs={{0,4},{4,8},{8,12},{12,16},{16,20},{20,24},{24,28},{28,32},{32,36}... | collective-permute-start | bytes 1032200 | tf_op jit(solution)/shard_map/ppermute | solution.py:127
  73.4 9.2 %collective-permute-start.4 = (bf16[224,768]{1,0:T(8,128)(2,1)S(1)}, bf16[224,768]{1,0:T(8,128)(2,1)S(1)}, u32[]{:S(2)}, u32[]{:S(2)}) collective-permute-start(bf16[224,768]{1,0:T(8,128)(2,1)S(1)} %fusion.2), channel_id=1, source_target_pairs={{0,4},{4,8},{8,12},{12,16},{16,20},{20,24},{24,28},{28,32},{32,36}... | collective-permute-start | bytes 1032200 | tf_op jit(solution)/shard_map/ppermute | solution.py:127
  79.2 10.8 %collective-permute-start.13 = (bf16[224,768]{1,0:T(8,128)(2,1)S(1)}, bf16[224,768]{1,0:T(8,128)(2,1)S(1)}, u32[]{:S(2)}, u32[]{:S(2)}) collective-permute-start(bf16[224,768]{1,0:T(8,128)(2,1)S(1)} %fusion.4), channel_id=1, source_target_pairs={{0,4},{4,8},{8,12},{12,16},{16,20},{20,24},{24,28},{28,32},{32,36}... | collective-permute-start | bytes 1032200 | tf_op jit(solution)/shard_map/ppermute | solution.py:127
  83.0 9.4 %collective-permute-start.5 = (bf16[224,768]{1,0:T(8,128)(2,1)S(1)}, bf16[224,768]{1,0:T(8,128)(2,1)S(1)}, u32[]{:S(2)}, u32[]{:S(2)}) collective-permute-start(bf16[224,768]{1,0:T(8,128)(2,1)S(1)} %fusion.1), channel_id=1, source_target_pairs={{0,4},{4,8},{8,12},{12,16},{16,20},{20,24},{24,28},{28,32},{32,36}... | collective-permute-start | bytes 1032200 | tf_op jit(solution)/shard_map/ppermute | solution.py:127
  88.5 1.5 copy-start.5
  90.5 8.3 %collective-permute-start.14 = (bf16[224,768]{1,0:T(8,128)(2,1)S(1)}, bf16[224,768]{1,0:T(8,128)(2,1)S(1)}, u32[]{:S(2)}, u32[]{:S(2)}) collective-permute-start(bf16[224,768]{1,0:T(8,128)(2,1)S(1)} %fusion.3), channel_id=1, source_target_pairs={{0,4},{4,8},{8,12},{12,16},{16,20},{20,24},{24,28},{28,32},{32,36}... | collective-permute-start | bytes 1032200 | tf_op jit(solution)/shard_map/ppermute | solution.py:127
  92.8 9.4 %collective-permute-start.6 = (bf16[224,768]{1,0:T(8,128)(2,1)S(1)}, bf16[224,768]{1,0:T(8,128)(2,1)S(1)}, u32[]{:S(2)}, u32[]{:S(2)}) collective-permute-start(bf16[224,768]{1,0:T(8,128)(2,1)S(1)} %fusion), channel_id=1, source_target_pairs={{0,4},{4,8},{8,12},{12,16},{16,20},{20,24},{24,28},{28,32},{32,36}... | collective-permute-start | bytes 1032200 | tf_op jit(solution)/shard_map/ppermute | solution.py:127
  98.8 8.4 %collective-permute-start.15 = (bf16[224,768]{1,0:T(8,128)(2,1)S(1)}, bf16[224,768]{1,0:T(8,128)(2,1)S(1)}, u32[]{:S(2)}, u32[]{:S(2)}) collective-permute-start(bf16[224,768]{1,0:T(8,128)(2,1)S(1)} %add_convert_fusion.3), channel_id=1, source_target_pairs={{0,4},{4,8},{8,12},{12,16},{16,20},{20,24},{24,28},{28,32},{32,36}... | collective-permute-start | bytes 1032200 | tf_op jit(solution)/shard_map/ppermute | solution.py:127
  102.2 8.8 %collective-permute-start.7 = (bf16[224,768]{1,0:T(8,128)(2,1)S(1)}, bf16[224,768]{1,0:T(8,128)(2,1)S(1)}, u32[]{:S(2)}, u32[]{:S(2)}) collective-permute-start(bf16[224,768]{1,0:T(8,128)(2,1)S(1)} %add_convert_fusion.7), channel_id=1, source_target_pairs={{0,4},{4,8},{8,12},{12,16},{16,20},{20,24},{24,28},{28,32},{32,36}... | collective-permute-start | bytes 1032200 | tf_op jit(solution)/shard_map/ppermute | solution.py:127
  107.3 9.2 %collective-permute-start.16 = (bf16[224,768]{1,0:T(8,128)(2,1)S(1)}, bf16[224,768]{1,0:T(8,128)(2,1)S(1)}, u32[]{:S(2)}, u32[]{:S(2)}) collective-permute-start(bf16[224,768]{1,0:T(8,128)(2,1)S(1)} %add_convert_fusion.2), channel_id=1, source_target_pairs={{0,4},{4,8},{8,12},{12,16},{16,20},{20,24},{24,28},{28,32},{32,36}... | collective-permute-start | bytes 1032200 | tf_op jit(solution)/shard_map/ppermute | solution.py:127
  111.1 9.2 %collective-permute-start.8 = (bf16[224,768]{1,0:T(8,128)(2,1)S(1)}, bf16[224,768]{1,0:T(8,128)(2,1)S(1)}, u32[]{:S(2)}, u32[]{:S(2)}) collective-permute-start(bf16[224,768]{1,0:T(8,128)(2,1)S(1)} %add_convert_fusion.6), channel_id=1, source_target_pairs={{0,4},{4,8},{8,12},{12,16},{16,20},{20,24},{24,28},{28,32},{32,36}... | collective-permute-start | bytes 1032200 | tf_op jit(solution)/shard_map/ppermute | solution.py:127
  116.6 9.2 %collective-permute-start.17 = (bf16[224,768]{1,0:T(8,128)(2,1)S(1)}, bf16[224,768]{1,0:T(8,128)(2,1)S(1)}, u32[]{:S(2)}, u32[]{:S(2)}) collective-permute-start(bf16[224,768]{1,0:T(8,128)(2,1)S(1)} %add_convert_fusion.1), channel_id=1, source_target_pairs={{0,4},{4,8},{8,12},{12,16},{16,20},{20,24},{24,28},{28,32},{32,36}... | collective-permute-start | bytes 1032200 | tf_op jit(solution)/shard_map/ppermute | solution.py:127
  120.4 9.2 %collective-permute-start.9 = (bf16[224,768]{1,0:T(8,128)(2,1)S(1)}, bf16[224,768]{1,0:T(8,128)(2,1)S(1)}, u32[]{:S(2)}, u32[]{:S(2)}) collective-permute-start(bf16[224,768]{1,0:T(8,128)(2,1)S(1)} %add_convert_fusion.5), channel_id=1, source_target_pairs={{0,4},{4,8},{8,12},{12,16},{16,20},{20,24},{24,28},{28,32},{32,36}... | collective-permute-start | bytes 1032200 | tf_op jit(solution)/shard_map/ppermute | solution.py:127
  126.6 5.3 %collective-permute-start.18 = (bf16[224,768]{1,0:T(8,128)(2,1)}, bf16[224,768]{1,0:T(8,128)(2,1)}, u32[]{:S(2)}, u32[]{:S(2)}) collective-permute-start(bf16[224,768]{1,0:T(8,128)(2,1)} %add_convert_fusion), channel_id=1, source_target_pairs={{0,4},{4,8},{8,12},{12,16},{16,20},{20,24},{24,28},{28,32},{32,36}... | collective-permute-start | bytes 1032200 | tf_op jit(solution)/shard_map/ppermute | solution.py:127
  129.6 24.3 %copy-start = (bf16[72,24576]{1,0:T(8,128)(2,1)S(1)}, bf16[72,24576]{1,0:T(8,128)(2,1)}, u32[]{:S(2)}) copy-start(bf16[72,24576]{1,0:T(8,128)(2,1)} %table_ref.2) | copy-start | bytes 10616836
  130.4 23.5 %copy-start.7 = (s32[448]{0:T(512)S(1)}, s32[448]{0:T(512)}, u32[]{:S(2)}) copy-start(s32[448]{0:T(512)} %param.8) | copy-start | bytes 5380
  130.4 2.6 %collective-permute-start.10 = (bf16[224,768]{1,0:T(8,128)(2,1)}, bf16[224,768]{1,0:T(8,128)(2,1)}, u32[]{:S(2)}, u32[]{:S(2)}) collective-permute-start(bf16[224,768]{1,0:T(8,128)(2,1)} %add_convert_fusion.4), channel_id=1, source_target_pairs={{0,4},{4,8},{8,12},{12,16},{16,20},{20,24},{24,28},{28,32},{32,36}... | collective-permute-start | bytes 1032200 | tf_op jit(solution)/shard_map/ppermute | solution.py:127
  132.9 1.2 copy-start.1
  134.1 0.8 copy-start.2
  135.0 29.0 %collective-permute-start.19 = (bf16[448,384]{1,0:T(8,128)(2,1)}, bf16[448,384]{1,0:T(8,128)(2,1)}, u32[]{:S(2)}, u32[]{:S(2)}) collective-permute-start(bf16[448,384]{1,0:T(8,128)(2,1)} %fusion.31), channel_id=1, source_target_pairs={{0,1},{1,0},{2,3},{3,2},{4,5},{5,4},{6,7},{7,6},{8,9},{9,8},{10,11... | collective-permute-start | bytes 1032200 | tf_op jit(solution)/shard_map/ppermute | solution.py:131
  166.2 15.3 %all-to-all-start.3 = ((f32[32,8,128]{2,1,0:T(8,128)}), f32[32,8,128]{2,1,0:T(8,128)S(1)}, u32[]{:S(2)}, u32[]{:S(2)}) async-start(f32[32,8,128]{2,1,0:T(8,128)} %broadcast_in_dim.81), calls=%async_computation.3 | async-start | bytes 262144 | tf_op jit(solution)/shard_map/all_to_all | solution.py:21
  182.3 14.6 %all-to-all-start = ((bf16[8,72,448]{2,1,0:T(8,128)(2,1)}), bf16[8,72,448]{2,1,0:T(8,128)(2,1)S(1)}, u32[]{:S(2)}, u32[]{:S(2)}) async-start(bf16[8,72,448]{2,1,0:T(8,128)(2,1)} %broadcast_in_dim.76), calls=%async_computation | async-start | bytes 1179648 | tf_op jit(solution)/shard_map/all_to_all | solution.py:21
  197.5 15.1 %all-to-all-start.4 = ((f32[16,8,128]{2,1,0:T(8,128)}), f32[16,8,128]{2,1,0:T(8,128)S(1)}, u32[]{:S(2)}, u32[]{:S(2)}) async-start(f32[16,8,128]{2,1,0:T(8,128)} %broadcast_in_dim.82), calls=%async_computation.4 | async-start | bytes 131072 | tf_op jit(solution)/shard_map/all_to_all | solution.py:21

commit v3 on v2

--- a/solution.py
+++ b/solution.py
@@ -135,9 +135,11 @@
     inside = jnp.logical_and(local_ids >= 0, local_ids < span_cols)
     found = jnp.take(late_table, jnp.clip(local_ids, 0, span_cols - 1), axis=1)
     found = jnp.where(inside[None, :], found, 0)
-    found = copies_of(found, GROUP).reshape(-1, share, tok)
-    embed = jnp.sum(found.astype(jnp.float32), axis=0)
-    next_embed = (embed * math.sqrt(width)).astype(jnp.bfloat16).T
+    for axis, bit in (("group_0", 1), ("group_0", 2), ("group_1", 1)):
+        pairs = [(q, q ^ bit) for q in range(lax.axis_size(axis))]
+        other = lax.ppermute(found, axis, pairs)
+        found = found + other
+    next_embed = (found.astype(jnp.float32) * math.sqrt(width)).astype(jnp.bfloat16).T
 
     capped = 30.0 * jnp.tanh(logits / 30.0)
     offsets = ids - (group_index * far_n * near_n + vocab_index) * voc_cols

time: 217 us -> 207 us (0.954)
  waiting for transfers between devices: 43.9 us -> 28 us
  matrix products: 8.84 us -> 22.9 us
  other arithmetic: 12 us -> 5.14 us
  starting transfers between devices: 112 us -> 109 us
    all_to_all x4 -> x3, waiting for transfers between devices: 39.4 us -> 21 us  [copies_of(): return lax.all_to_all(many, axes, split_axis=0, concat_axis=0, tiled=True)]
    dot_general x16, matrix products: 8.84 us -> 22.9 us  [layer(): jnp.dot(normed[h * rows:(h + 1) * rows], w, preferred_element_type=jnp.fl...]
    ppermute x0 -> x3, starting transfers between devices: none -> 12.5 us  [layer(): other = lax.ppermute(found, axis, pairs)]
    ppermute x16, starting transfers between devices: 56.5 us -> 45.2 us  [layer(): came[h] = lax.ppermute(out[h], (FAR, 'core'), onward(j))]
    ppermute x1, starting transfers between devices: 18.9 us -> 11.8 us  [layer(): given = lax.ppermute(given, 'core', [(0, 1), (1, 0)])]
    ppermute x0 -> x3, waiting for transfers between devices: none -> 3.09 us  [layer(): other = lax.ppermute(found, axis, pairs)]
    all_to_all x4 -> x3, starting transfers between devices: 24.3 us -> 25.5 us  [copies_of(): return lax.all_to_all(many, axes, split_axis=0, concat_axis=0, tiled=True)]
  transfers between devices with their start and end apart: 25 -> 27, of which waited for: 12 -> 5; matrix products, arithmetic and copies ran while one was open for 12% -> 19% of each run, Pallas kernels for 2% -> 2%
where the time goes in v3:
time: 207 us; the launch traced here: 204 us
  starting transfers between devices  109 us (53%)
  waiting for transfers between devices  28 us (14%)
  matrix products  22.9 us (11%)
  local copies, waits for them, and re-layouts  17.2 us (8%)
  blocking collectives  12.5 us (6%)
  Pallas kernels  7.08 us (3%)
  other arithmetic  5.14 us (2%)
    ppermute x16, starting transfers between devices, layer(): came[h] = lax.ppermute(out[h], (FAR, 'core'), onward(j))  45.2 us
    all_to_all x3, starting transfers between devices, copies_of(): return lax.all_to_all(many, axes, split_axis=0, concat_axis=0, tiled=True)  25.5 us
    dot_general x16, matrix products, layer(): jnp.dot(normed[h * rows:(h + 1) * rows], w, preferred_element_type=jnp.fl...  22.9 us
    all_to_all x3, waiting for transfers between devices, copies_of(): return lax.all_to_all(many, axes, split_axis=0, concat_axis=0, tiled=True)  21 us
    all_gather x1, blocking collectives, layer(): both = lax.all_gather(both, NEAR, axis=0, tiled=True)  12.5 us
    ppermute x3, starting transfers between devices, layer(): other = lax.ppermute(found, axis, pairs)  12.5 us
    ppermute x1, starting transfers between devices, layer(): given = lax.ppermute(given, 'core', [(0, 1), (1, 0)])  11.8 us
    ppermute x3, starting transfers between devices, layer(): slab = lax.ppermute(slab, NEAR, [(i, i ^ k) for i in range(near_n)])  7.87 us
  transfers between devices with their start and end apart: 27, of which 5 were waited for; matrix products, arithmetic and copies ran while one was open for 19% of the time, Pallas kernels for 2%

profile of v3, /device:TPU:1, one launch (start us, length us, event | category | flops | bytes accessed | tf_op | source)
XLA Modules:
  0.0 203.7 jit_solution(17302670699822056355)
XLA Ops:
  0.6 0.7 and_select_fusion
  1.4 0.6 reshape.45.places_ref
  2.0 0.7 broadcast_in_dim.66
  2.7 1.0 pad_maximum_fusion
  3.7 12.5 %all_gather.3 = bf16[288,512]{1,0:T(8,128)(2,1)S(1)} all-gather(bf16[72,512]{1,0:T(8,128)(2,1)S(1)} %pad_maximum_fusion), channel_id=1, replica_groups=mesh['group_0'=4,'group_1'=2,'depth'=16,'row'=2,'core'=2] {'row','core'}, dimensions={0}, use_global_device_ids=true | all-gather | bytes 368640 | tf_op jit(solution)/shard_map/all_gather | solution.py:88
  16.2 3.5 %shard_map.76 = (bf16[72,3072]{1,0:T(8,128)(2,1)}, bf16[72,3072]{1,0:T(8,128)(2,1)}, bf16[72,3072]{1,0:T(8,128)(2,1)}, bf16[72,3072]{1,0:T(8,128)(2,1)}) custom-call(s32[8]{0:T(128)} %reshape.45.places_ref, s32[1]{0:T(128)} %bitcast.near_ref, bf16[72,24576]{1,0:T(8,128)(2,1)} %table_ref.2), custom_call_target="tpu_custom_call" | custom-call | tf_op jit(solution)/shard_map/pallas_call | solution.py:56
  19.8 2.1 %collective-permute-start.3 = (bf16[72,3072]{1,0:T(8,128)(2,1)}, bf16[72,3072]{1,0:T(8,128)(2,1)}, u32[]{:S(2)}, u32[]{:S(2)}) collective-permute-start(bf16[72,3072]{1,0:T(8,128)(2,1)} %get-tuple-element.22), channel_id=1, source_target_pairs={{0,1},{1,0},{2,3},{3,2},{4,5},{5,4},{6,7},{7,6},{8,9},{9,8},{10,11... | collective-permute-start | bytes 1327112 | tf_op jit(solution)/shard_map/ppermute | solution.py:94
  21.8 2.2 %collective-permute-start.4 = (bf16[72,3072]{1,0:T(8,128)(2,1)}, bf16[72,3072]{1,0:T(8,128)(2,1)S(1)}, u32[]{:S(2)}, u32[]{:S(2)}) collective-permute-start(bf16[72,3072]{1,0:T(8,128)(2,1)} %get-tuple-element.23), channel_id=1, source_target_pairs={{0,2},{1,3},{2,0},{3,1},{4,6},{5,7},{6,4},{7,5},{8,10},{9,11},{10,... | collective-permute-start | bytes 1327112 | tf_op jit(solution)/shard_map/ppermute | solution.py:94
  24.1 3.6 %collective-permute-start.5 = (bf16[72,3072]{1,0:T(8,128)(2,1)}, bf16[72,3072]{1,0:T(8,128)(2,1)S(1)}, u32[]{:S(2)}, u32[]{:S(2)}) collective-permute-start(bf16[72,3072]{1,0:T(8,128)(2,1)} %get-tuple-element.24), channel_id=1, source_target_pairs={{0,3},{1,2},{2,1},{3,0},{4,7},{5,6},{6,5},{7,4},{8,11},{9,10},{10,... | collective-permute-start | bytes 1327112 | tf_op jit(solution)/shard_map/ppermute | solution.py:94
  27.8 0.6 broadcast_in_dim.71
  28.4 9.7 %all-to-all-start = ((f32[16,4,128]{2,1,0:T(4,128)}), f32[16,4,128]{2,1,0:T(4,128)S(1)}, u32[]{:S(2)}, u32[]{:S(2)}) async-start(f32[16,4,128]{2,1,0:T(4,128)} %broadcast_in_dim.71), calls=%async_computation | async-start | bytes 65536 | tf_op jit(solution)/shard_map/all_to_all | solution.py:21
  38.4 0.8 copy-done.5
  39.4 10.2 %all-to-all-done = f32[16,4,128]{2,1,0:T(4,128)S(1)} async-done(((f32[16,4,128]{2,1,0:T(4,128)}), f32[16,4,128]{2,1,0:T(4,128)S(1)}, u32[]{:S(2)}, u32[]{:S(2)}) %all-to-all-start) | async-done | bytes 32800 | tf_op jit(solution)/shard_map/all_to_all | solution.py:21
  49.8 1.2 constant_dynamic-update-slice_fusion.2
  51.1 1.3 convolution_convert_fusion
  52.4 2.7 %collective-permute-start.14 = (bf16[224,768]{1,0:T(8,128)(2,1)}, bf16[224,768]{1,0:T(8,128)(2,1)}, u32[]{:S(2)}, u32[]{:S(2)}) collective-permute-start(bf16[224,768]{1,0:T(8,128)(2,1)} %convolution_convert_fusion), channel_id=1, source_target_pairs={{0,4},{4,8},{8,12},{12,16},{16,20},{20,24},{24,28},{28,32},{32,36}... | collective-permute-start | bytes 1032200 | tf_op jit(solution)/shard_map/ppermute | solution.py:127
  55.2 1.1 convolution_convert_fusion.1
  56.3 1.9 collective-permute-start.6
  58.2 0.6 reshape.47.places_ref
  58.8 3.5 %shard_map.77 = bf16[4,72,3072]{2,1,0:T(8,128)(2,1)} custom-call(s32[8]{0:T(128)} %reshape.47.places_ref, s32[1]{0:T(128)} %constant.84.clone.1.near_ref, bf16[72,24576]{1,0:T(8,128)(2,1)} %table_ref.2), custom_call_target="tpu_custom_call" | custom-call | tf_op jit(solution)/shard_map/pallas_call | solution.py:56
  62.4 6.6 %all-to-all-start.1 = ((bf16[4,72,3072]{2,1,0:T(8,128)(2,1)}), bf16[4,72,3072]{2,1,0:T(8,128)(2,1)}, u32[]{:S(2)}, u32[]{:S(2)}) async-start(bf16[4,72,3072]{2,1,0:T(8,128)(2,1)} %shard_map.77), calls=%async_computation.1 | async-start | bytes 3538944 | tf_op jit(solution)/shard_map/all_to_all | solution.py:107
  69.0 2.4 %fusion.5 = bf16[224,768]{1,0:T(8,128)(2,1)} fusion(bf16[224,768]{1,0:T(8,128)(2,1)} %collective-permute-done.14, bf16[288,3072]{1,0:T(8,128)(2,1)} %copy-done.3, bf16[448,288]{0,1:T(8,128)(2,1)} %copy-done.1), kind=kOutput, calls=%fused_computation.12 | convolution fusion | flops 99606528 | bytes 1277952 | tf_op jit(solution)/shard_map/dot_general | solution.py:123
  71.4 4.1 %collective-permute-start.15 = (bf16[224,768]{1,0:T(8,128)(2,1)}, bf16[224,768]{1,0:T(8,128)(2,1)}, u32[]{:S(2)}, u32[]{:S(2)}) collective-permute-start(bf16[224,768]{1,0:T(8,128)(2,1)} %fusion.5), channel_id=1, source_target_pairs={{0,4},{4,8},{8,12},{12,16},{16,20},{20,24},{24,28},{28,32},{32,36}... | collective-permute-start | bytes 1032200 | tf_op jit(solution)/shard_map/ppermute | solution.py:127
  75.6 2.3 %fusion.2 = bf16[224,768]{1,0:T(8,128)(2,1)} fusion(bf16[224,768]{1,0:T(8,128)(2,1)} %collective-permute-done.6, bf16[288,3072]{1,0:T(8,128)(2,1)} %copy-done.3, bf16[448,288]{0,1:T(8,128)(2,1)} %copy-done.1), kind=kOutput, calls=%fused_computation.9 | convolution fusion | flops 99606528 | bytes 1277952 | tf_op jit(solution)/shard_map/dot_general | solution.py:123
  77.8 3.0 %collective-permute-start.7 = (bf16[224,768]{1,0:T(8,128)(2,1)}, bf16[224,768]{1,0:T(8,128)(2,1)}, u32[]{:S(2)}, u32[]{:S(2)}) collective-permute-start(bf16[224,768]{1,0:T(8,128)(2,1)} %fusion.2), channel_id=1, source_target_pairs={{0,4},{4,8},{8,12},{12,16},{16,20},{20,24},{24,28},{28,32},{32,36}... | collective-permute-start | bytes 1032200 | tf_op jit(solution)/shard_map/ppermute | solution.py:127
  80.9 5.2 %copy.14 = bf16[72,24576]{0,1:T(8,128)(2,1)} copy(bf16[72,24576]{1,0:T(8,128)(2,1)S(1)} %copy-done) | data formatting | bytes 7077888 | tf_op jit(solution)/shard_map/optimization_barrier | solution.py:101
  86.2 1.7 fusion.4
  87.9 1.9 collective-permute-start.16
  89.8 1.6 fusion.1
  91.4 1.9 collective-permute-start.8
  93.3 1.5 fusion.14
  94.8 1.6 fusion.18
  96.5 1.5 fusion.22
  97.9 1.5 fusion.26
  99.9 3.1 %collective-permute-start.17 = (bf16[224,768]{1,0:T(8,128)(2,1)S(1)}, bf16[224,768]{1,0:T(8,128)(2,1)S(1)}, u32[]{:S(2)}, u32[]{:S(2)}) collective-permute-start(bf16[224,768]{1,0:T(8,128)(2,1)S(1)} %fusion.3), channel_id=1, source_target_pairs={{0,4},{4,8},{8,12},{12,16},{16,20},{20,24},{24,28},{28,32},{32,36}... | collective-permute-start | bytes 1032200 | tf_op jit(solution)/shard_map/ppermute | solution.py:127
  103.4 2.1 %collective-permute-start.9 = (bf16[224,768]{1,0:T(8,128)(2,1)S(1)}, bf16[224,768]{1,0:T(8,128)(2,1)S(1)}, u32[]{:S(2)}, u32[]{:S(2)}) collective-permute-start(bf16[224,768]{1,0:T(8,128)(2,1)S(1)} %fusion), channel_id=1, source_target_pairs={{0,4},{4,8},{8,12},{12,16},{16,20},{20,24},{24,28},{28,32},{32,36}... | collective-permute-start | bytes 1032200 | tf_op jit(solution)/shard_map/ppermute | solution.py:127
  105.5 1.4 fusion.16
  106.9 1.3 collective-permute-done.17
  108.3 4.0 %collective-permute-start.18 = (bf16[224,768]{1,0:T(8,128)(2,1)S(1)}, bf16[224,768]{1,0:T(8,128)(2,1)S(1)}, u32[]{:S(2)}, u32[]{:S(2)}) collective-permute-start(bf16[224,768]{1,0:T(8,128)(2,1)S(1)} %add_convert_fusion.3), channel_id=1, source_target_pairs={{0,4},{4,8},{8,12},{12,16},{16,20},{20,24},{24,28},{28,32},{32,36}... | collective-permute-start | bytes 1032200 | tf_op jit(solution)/shard_map/ppermute | solution.py:127
  112.4 3.6 %collective-permute-start.10 = (bf16[224,768]{1,0:T(8,128)(2,1)S(1)}, bf16[224,768]{1,0:T(8,128)(2,1)S(1)}, u32[]{:S(2)}, u32[]{:S(2)}) collective-permute-start(bf16[224,768]{1,0:T(8,128)(2,1)S(1)} %add_convert_fusion.7), channel_id=1, source_target_pairs={{0,4},{4,8},{8,12},{12,16},{16,20},{20,24},{24,28},{28,32},{32,36}... | collective-permute-start | bytes 1032200 | tf_op jit(solution)/shard_map/ppermute | solution.py:127
  116.0 1.4 fusion.20
  117.4 4.1 %collective-permute-start.19 = (bf16[224,768]{1,0:T(8,128)(2,1)S(1)}, bf16[224,768]{1,0:T(8,128)(2,1)S(1)}, u32[]{:S(2)}, u32[]{:S(2)}) collective-permute-start(bf16[224,768]{1,0:T(8,128)(2,1)S(1)} %add_convert_fusion.2), channel_id=1, source_target_pairs={{0,4},{4,8},{8,12},{12,16},{16,20},{20,24},{24,28},{28,32},{32,36}... | collective-permute-start | bytes 1032200 | tf_op jit(solution)/shard_map/ppermute | solution.py:127
  121.6 3.6 %collective-permute-start.11 = (bf16[224,768]{1,0:T(8,128)(2,1)S(1)}, bf16[224,768]{1,0:T(8,128)(2,1)S(1)}, u32[]{:S(2)}, u32[]{:S(2)}) collective-permute-start(bf16[224,768]{1,0:T(8,128)(2,1)S(1)} %add_convert_fusion.6), channel_id=1, source_target_pairs={{0,4},{4,8},{8,12},{12,16},{16,20},{20,24},{24,28},{28,32},{32,36}... | collective-permute-start | bytes 1032200 | tf_op jit(solution)/shard_map/ppermute | solution.py:127
  125.3 1.4 fusion.24
  126.7 4.1 %collective-permute-start.20 = (bf16[224,768]{1,0:T(8,128)(2,1)S(1)}, bf16[224,768]{1,0:T(8,128)(2,1)S(1)}, u32[]{:S(2)}, u32[]{:S(2)}) collective-permute-start(bf16[224,768]{1,0:T(8,128)(2,1)S(1)} %add_convert_fusion.1), channel_id=1, source_target_pairs={{0,4},{4,8},{8,12},{12,16},{16,20},{20,24},{24,28},{28,32},{32,36}... | collective-permute-start | bytes 1032200 | tf_op jit(solution)/shard_map/ppermute | solution.py:127
  130.9 3.6 %collective-permute-start.12 = (bf16[224,768]{1,0:T(8,128)(2,1)S(1)}, bf16[224,768]{1,0:T(8,128)(2,1)S(1)}, u32[]{:S(2)}, u32[]{:S(2)}) collective-permute-start(bf16[224,768]{1,0:T(8,128)(2,1)S(1)} %add_convert_fusion.5), channel_id=1, source_target_pairs={{0,4},{4,8},{8,12},{12,16},{16,20},{20,24},{24,28},{28,32},{32,36}... | collective-permute-start | bytes 1032200 | tf_op jit(solution)/shard_map/ppermute | solution.py:127
  134.5 1.4 fusion.28
  136.0 0.7 collective-permute-start.21
  136.7 2.5 %collective-permute-done.12 = bf16[224,768]{1,0:T(8,128)(2,1)S(1)} collective-permute-done((bf16[224,768]{1,0:T(8,128)(2,1)S(1)}, bf16[224,768]{1,0:T(8,128)(2,1)S(1)}, u32[]{:S(2)}, u32[]{:S(2)}) %collective-permute-start.12) | collective-permute-done | bytes 344096 | tf_op jit(solution)/shard_map/ppermute | solution.py:127
  139.3 0.7 collective-permute-start.13
  140.0 4.8 %gather_fusion = bf16[448,72]{1,0:T(8,128)(2,1)S(1)} fusion(bf16[72,24576]{0,1:T(8,128)(2,1)} %copy.14, s32[1024]{0:T(1024)S(1)} %pad_clamp_fusion), kind=kCustom, calls=%fused_computation | custom fusion | bytes 130816 | tf_op jit(solution)/shard_map/jit(_take)/gather | solution.py:136
  145.0 11.8 %collective-permute-start.22 = (bf16[448,384]{1,0:T(8,128)(2,1)S(1)}, bf16[448,384]{1,0:T(8,128)(2,1)S(1)}, u32[]{:S(2)}, u32[]{:S(2)}) collective-permute-start(bf16[448,384]{1,0:T(8,128)(2,1)S(1)} %fusion.31), channel_id=1, source_target_pairs={{0,1},{1,0},{2,3},{3,2},{4,5},{5,4},{6,7},{7,6},{8,9},{9,8},{10,11... | collective-permute-start | bytes 1032200 | tf_op jit(solution)/shard_map/ppermute | solution.py:131
  157.0 3.1 %collective-permute-start = (bf16[72,448]{0,1:T(8,128)(2,1)S(1)}, bf16[72,448]{0,1:T(8,128)(2,1)S(1)}, u32[]{:S(2)}, u32[]{:S(2)}) collective-permute-start(bf16[72,448]{0,1:T(8,128)(2,1)S(1)} %select_bitcast_fusion), channel_id=1, source_target_pairs={{0,128},{128,0},{256,384},{384,256},{1,129},{129,1},{257,385},{385... | collective-permute-start | bytes 193544 | tf_op jit(solution)/shard_map/ppermute | solution.py:140
  160.6 0.7 broadcast_in_dim.74
  161.3 7.4 %all-to-all-start.2 = ((f32[32,8,128]{2,1,0:T(8,128)}), f32[32,8,128]{2,1,0:T(8,128)S(1)}, u32[]{:S(2)}, u32[]{:S(2)}) async-start(f32[32,8,128]{2,1,0:T(8,128)} %broadcast_in_dim.74), calls=%async_computation.2 | async-start | bytes 262144 | tf_op jit(solution)/shard_map/all_to_all | solution.py:21
  168.9 4.8 %collective-permute-start.1 = (bf16[72,448]{0,1:T(8,128)(2,1)S(1)}, bf16[72,448]{0,1:T(8,128)(2,1)S(1)}, u32[]{:S(2)}, u32[]{:S(2)}) collective-permute-start(bf16[72,448]{0,1:T(8,128)(2,1)S(1)} %fusion.55), channel_id=1, source_target_pairs={{0,256},{128,384},{256,0},{384,128},{1,257},{129,385},{257,1},{385... | collective-permute-start | bytes 193544 | tf_op jit(solution)/shard_map/ppermute | solution.py:140
  173.7 3.1 %collective-permute-done.1 = bf16[72,448]{0,1:T(8,128)(2,1)S(1)} collective-permute-done((bf16[72,448]{0,1:T(8,128)(2,1)S(1)}, bf16[72,448]{0,1:T(8,128)(2,1)S(1)}, u32[]{:S(2)}, u32[]{:S(2)}) %collective-permute-start.1) | collective-permute-done | bytes 64544 | tf_op jit(solution)/shard_map/ppermute | solution.py:140
  176.8 4.6 %collective-permute-start.2 = (bf16[72,448]{0,1:T(8,128)(2,1)S(1)}, bf16[72,448]{0,1:T(8,128)(2,1)S(1)}, u32[]{:S(2)}, u32[]{:S(2)}) collective-permute-start(bf16[72,448]{0,1:T(8,128)(2,1)S(1)} %add.122), channel_id=1, source_target_pairs={{0,64},{64,0},{1,65},{65,1},{2,66},{66,2},{3,67},{67,3},{4,68},{68... | collective-permute-start | bytes 193544 | tf_op jit(solution)/shard_map/ppermute | solution.py:140
  181.5 0.6 broadcast_in_dim.75
  182.1 8.3 %all-to-all-start.3 = ((f32[16,8,128]{2,1,0:T(8,128)}), f32[16,8,128]{2,1,0:T(8,128)S(1)}, u32[]{:S(2)}, u32[]{:S(2)}) async-start(f32[16,8,128]{2,1,0:T(8,128)} %broadcast_in_dim.75), calls=%async_computation.3 | async-start | bytes 131072 | tf_op jit(solution)/shard_map/all_to_all | solution.py:21
  190.5 0.7 copy.16
  191.2 10.8 %all-to-all-done.3 = f32[16,8,128]{2,1,0:T(8,128)S(1)} async-done(((f32[16,8,128]{2,1,0:T(8,128)}), f32[16,8,128]{2,1,0:T(8,128)S(1)}, u32[]{:S(2)}, u32[]{:S(2)}) %all-to-all-start.3) | async-done | bytes 65568 | tf_op jit(solution)/shard_map/all_to_all | solution.py:21
  202.1 0.6 sub.33
  202.7 1.0 fusion.30
  (74 shorter events, 3.4 us)
Async XLA Ops:
  19.8 30.0 %collective-permute-start.3 = (bf16[72,3072]{1,0:T(8,128)(2,1)}, bf16[72,3072]{1,0:T(8,128)(2,1)}, u32[]{:S(2)}, u32[]{:S(2)}) collective-permute-start(bf16[72,3072]{1,0:T(8,128)(2,1)} %get-tuple-element.22), channel_id=1, source_target_pairs={{0,1},{1,0},{2,3},{3,2},{4,5},{5,4},{6,7},{7,6},{8,9},{9,8},{10,11... | collective-permute-start | bytes 1327112 | tf_op jit(solution)/shard_map/ppermute | solution.py:94
  21.8 29.1 %collective-permute-start.4 = (bf16[72,3072]{1,0:T(8,128)(2,1)}, bf16[72,3072]{1,0:T(8,128)(2,1)S(1)}, u32[]{:S(2)}, u32[]{:S(2)}) collective-permute-start(bf16[72,3072]{1,0:T(8,128)(2,1)} %get-tuple-element.23), channel_id=1, source_target_pairs={{0,2},{1,3},{2,0},{3,1},{4,6},{5,7},{6,4},{7,5},{8,10},{9,11},{10,... | collective-permute-start | bytes 1327112 | tf_op jit(solution)/shard_map/ppermute | solution.py:94
  24.1 27.0 %collective-permute-start.5 = (bf16[72,3072]{1,0:T(8,128)(2,1)}, bf16[72,3072]{1,0:T(8,128)(2,1)S(1)}, u32[]{:S(2)}, u32[]{:S(2)}) collective-permute-start(bf16[72,3072]{1,0:T(8,128)(2,1)} %get-tuple-element.24), channel_id=1, source_target_pairs={{0,3},{1,2},{2,1},{3,0},{4,7},{5,6},{6,5},{7,4},{8,11},{9,10},{10,... | collective-permute-start | bytes 1327112 | tf_op jit(solution)/shard_map/ppermute | solution.py:94
  28.4 21.2 %all-to-all-start = ((f32[16,4,128]{2,1,0:T(4,128)}), f32[16,4,128]{2,1,0:T(4,128)S(1)}, u32[]{:S(2)}, u32[]{:S(2)}) async-start(f32[16,4,128]{2,1,0:T(4,128)} %broadcast_in_dim.71), calls=%async_computation | async-start | bytes 65536 | tf_op jit(solution)/shard_map/all_to_all | solution.py:21
  38.2 1.0 copy-start.5
  49.8 5.4 %copy-start.1 = (bf16[448,288]{0,1:T(8,128)(2,1)}, bf16[448,288]{0,1:T(8,128)(2,1)S(1)}, u32[]{:S(2)}) copy-start(bf16[448,288]{0,1:T(8,128)(2,1)S(1)} %fusion.33) | copy-start | bytes 774148
  51.1 7.7 %copy-start.3 = (bf16[288,3072]{1,0:T(8,128)(2,1)}, bf16[288,3072]{1,0:T(8,128)(2,1)S(1)}, u32[]{:S(2)}) copy-start(bf16[288,3072]{1,0:T(8,128)(2,1)S(1)} %constant_dynamic-update-slice_fusion) | copy-start | bytes 5308420
  52.4 16.5 %collective-permute-start.14 = (bf16[224,768]{1,0:T(8,128)(2,1)}, bf16[224,768]{1,0:T(8,128)(2,1)}, u32[]{:S(2)}, u32[]{:S(2)}) collective-permute-start(bf16[224,768]{1,0:T(8,128)(2,1)} %convolution_convert_fusion), channel_id=1, source_target_pairs={{0,4},{4,8},{8,12},{12,16},{16,20},{20,24},{24,28},{28,32},{32,36}... | collective-permute-start | bytes 1032200 | tf_op jit(solution)/shard_map/ppermute | solution.py:127
  56.3 19.2 %collective-permute-start.6 = (bf16[224,768]{1,0:T(8,128)(2,1)}, bf16[224,768]{1,0:T(8,128)(2,1)}, u32[]{:S(2)}, u32[]{:S(2)}) collective-permute-start(bf16[224,768]{1,0:T(8,128)(2,1)} %convolution_convert_fusion.1), channel_id=1, source_target_pairs={{0,4},{4,8},{8,12},{12,16},{16,20},{20,24},{24,28},{28,32},{32,36}... | collective-permute-start | bytes 1032200 | tf_op jit(solution)/shard_map/ppermute | solution.py:127
  62.4 18.5 %copy-start = (bf16[72,24576]{1,0:T(8,128)(2,1)S(1)}, bf16[72,24576]{1,0:T(8,128)(2,1)}, u32[]{:S(2)}) copy-start(bf16[72,24576]{1,0:T(8,128)(2,1)} %table_ref.2) | copy-start | bytes 10616836
  62.4 30.9 %all-to-all-start.1 = ((bf16[4,72,3072]{2,1,0:T(8,128)(2,1)}), bf16[4,72,3072]{2,1,0:T(8,128)(2,1)}, u32[]{:S(2)}, u32[]{:S(2)}) async-start(bf16[4,72,3072]{2,1,0:T(8,128)(2,1)} %shard_map.77), calls=%async_computation.1 | async-start | bytes 3538944 | tf_op jit(solution)/shard_map/all_to_all | solution.py:107
  69.0 11.9 %copy-start.6 = (s32[448]{0:T(512)S(1)}, s32[448]{0:T(512)}, u32[]{:S(2)}) copy-start(s32[448]{0:T(512)} %param.8) | copy-start | bytes 5380
  71.4 14.7 %collective-permute-start.15 = (bf16[224,768]{1,0:T(8,128)(2,1)}, bf16[224,768]{1,0:T(8,128)(2,1)}, u32[]{:S(2)}, u32[]{:S(2)}) collective-permute-start(bf16[224,768]{1,0:T(8,128)(2,1)} %fusion.5), channel_id=1, source_target_pairs={{0,4},{4,8},{8,12},{12,16},{16,20},{20,24},{24,28},{28,32},{32,36}... | collective-permute-start | bytes 1032200 | tf_op jit(solution)/shard_map/ppermute | solution.py:127
  77.8 12.0 %collective-permute-start.7 = (bf16[224,768]{1,0:T(8,128)(2,1)}, bf16[224,768]{1,0:T(8,128)(2,1)}, u32[]{:S(2)}, u32[]{:S(2)}) collective-permute-start(bf16[224,768]{1,0:T(8,128)(2,1)} %fusion.2), channel_id=1, source_target_pairs={{0,4},{4,8},{8,12},{12,16},{16,20},{20,24},{24,28},{28,32},{32,36}... | collective-permute-start | bytes 1032200 | tf_op jit(solution)/shard_map/ppermute | solution.py:127
  86.2 7.2 %copy-start.2 = (bf16[448,288]{0,1:T(8,128)(2,1)S(1)}, bf16[448,288]{0,1:T(8,128)(2,1)}, u32[]{:S(2)}) copy-start(bf16[448,288]{0,1:T(8,128)(2,1)} %copy-done.1) | copy-start | bytes 774148
  87.9 11.5 %collective-permute-start.16 = (bf16[224,768]{1,0:T(8,128)(2,1)S(1)}, bf16[224,768]{1,0:T(8,128)(2,1)S(1)}, u32[]{:S(2)}, u32[]{:S(2)}) collective-permute-start(bf16[224,768]{1,0:T(8,128)(2,1)S(1)} %fusion.4), channel_id=1, source_target_pairs={{0,4},{4,8},{8,12},{12,16},{16,20},{20,24},{24,28},{28,32},{32,36}... | collective-permute-start | bytes 1032200 | tf_op jit(solution)/shard_map/ppermute | solution.py:127
  91.4 11.6 %collective-permute-start.8 = (bf16[224,768]{1,0:T(8,128)(2,1)S(1)}, bf16[224,768]{1,0:T(8,128)(2,1)S(1)}, u32[]{:S(2)}, u32[]{:S(2)}) collective-permute-start(bf16[224,768]{1,0:T(8,128)(2,1)S(1)} %fusion.1), channel_id=1, source_target_pairs={{0,4},{4,8},{8,12},{12,16},{16,20},{20,24},{24,28},{28,32},{32,36}... | collective-permute-start | bytes 1032200 | tf_op jit(solution)/shard_map/ppermute | solution.py:127
  94.8 4.6 %copy-start.4 = (bf16[288,3072]{1,0:T(8,128)(2,1)S(1)}, bf16[288,3072]{1,0:T(8,128)(2,1)}, u32[]{:S(2)}) copy-start(bf16[288,3072]{1,0:T(8,128)(2,1)} %copy-done.3) | copy-start | bytes 5308420
  99.9 8.3 %collective-permute-start.17 = (bf16[224,768]{1,0:T(8,128)(2,1)S(1)}, bf16[224,768]{1,0:T(8,128)(2,1)S(1)}, u32[]{:S(2)}, u32[]{:S(2)}) collective-permute-start(bf16[224,768]{1,0:T(8,128)(2,1)S(1)} %fusion.3), channel_id=1, source_target_pairs={{0,4},{4,8},{8,12},{12,16},{16,20},{20,24},{24,28},{28,32},{32,36}... | collective-permute-start | bytes 1032200 | tf_op jit(solution)/shard_map/ppermute | solution.py:127
  103.4 8.9 %collective-permute-start.9 = (bf16[224,768]{1,0:T(8,128)(2,1)S(1)}, bf16[224,768]{1,0:T(8,128)(2,1)S(1)}, u32[]{:S(2)}, u32[]{:S(2)}) collective-permute-start(bf16[224,768]{1,0:T(8,128)(2,1)S(1)} %fusion), channel_id=1, source_target_pairs={{0,4},{4,8},{8,12},{12,16},{16,20},{20,24},{24,28},{28,32},{32,36}... | collective-permute-start | bytes 1032200 | tf_op jit(solution)/shard_map/ppermute | solution.py:127
  108.3 9.1 %collective-permute-start.18 = (bf16[224,768]{1,0:T(8,128)(2,1)S(1)}, bf16[224,768]{1,0:T(8,128)(2,1)S(1)}, u32[]{:S(2)}, u32[]{:S(2)}) collective-permute-start(bf16[224,768]{1,0:T(8,128)(2,1)S(1)} %add_convert_fusion.3), channel_id=1, source_target_pairs={{0,4},{4,8},{8,12},{12,16},{16,20},{20,24},{24,28},{28,32},{32,36}... | collective-permute-start | bytes 1032200 | tf_op jit(solution)/shard_map/ppermute | solution.py:127
  112.4 9.2 %collective-permute-start.10 = (bf16[224,768]{1,0:T(8,128)(2,1)S(1)}, bf16[224,768]{1,0:T(8,128)(2,1)S(1)}, u32[]{:S(2)}, u32[]{:S(2)}) collective-permute-start(bf16[224,768]{1,0:T(8,128)(2,1)S(1)} %add_convert_fusion.7), channel_id=1, source_target_pairs={{0,4},{4,8},{8,12},{12,16},{16,20},{20,24},{24,28},{28,32},{32,36}... | collective-permute-start | bytes 1032200 | tf_op jit(solution)/shard_map/ppermute | solution.py:127
  117.4 9.2 %collective-permute-start.19 = (bf16[224,768]{1,0:T(8,128)(2,1)S(1)}, bf16[224,768]{1,0:T(8,128)(2,1)S(1)}, u32[]{:S(2)}, u32[]{:S(2)}) collective-permute-start(bf16[224,768]{1,0:T(8,128)(2,1)S(1)} %add_convert_fusion.2), channel_id=1, source_target_pairs={{0,4},{4,8},{8,12},{12,16},{16,20},{20,24},{24,28},{28,32},{32,36}... | collective-permute-start | bytes 1032200 | tf_op jit(solution)/shard_map/ppermute | solution.py:127
  121.6 9.2 %collective-permute-start.11 = (bf16[224,768]{1,0:T(8,128)(2,1)S(1)}, bf16[224,768]{1,0:T(8,128)(2,1)S(1)}, u32[]{:S(2)}, u32[]{:S(2)}) collective-permute-start(bf16[224,768]{1,0:T(8,128)(2,1)S(1)} %add_convert_fusion.6), channel_id=1, source_target_pairs={{0,4},{4,8},{8,12},{12,16},{16,20},{20,24},{24,28},{28,32},{32,36}... | collective-permute-start | bytes 1032200 | tf_op jit(solution)/shard_map/ppermute | solution.py:127
  126.7 9.2 %collective-permute-start.20 = (bf16[224,768]{1,0:T(8,128)(2,1)S(1)}, bf16[224,768]{1,0:T(8,128)(2,1)S(1)}, u32[]{:S(2)}, u32[]{:S(2)}) collective-permute-start(bf16[224,768]{1,0:T(8,128)(2,1)S(1)} %add_convert_fusion.1), channel_id=1, source_target_pairs={{0,4},{4,8},{8,12},{12,16},{16,20},{20,24},{24,28},{28,32},{32,36}... | collective-permute-start | bytes 1032200 | tf_op jit(solution)/shard_map/ppermute | solution.py:127
  130.9 8.3 %collective-permute-start.12 = (bf16[224,768]{1,0:T(8,128)(2,1)S(1)}, bf16[224,768]{1,0:T(8,128)(2,1)S(1)}, u32[]{:S(2)}, u32[]{:S(2)}) collective-permute-start(bf16[224,768]{1,0:T(8,128)(2,1)S(1)} %add_convert_fusion.5), channel_id=1, source_target_pairs={{0,4},{4,8},{8,12},{12,16},{16,20},{20,24},{24,28},{28,32},{32,36}... | collective-permute-start | bytes 1032200 | tf_op jit(solution)/shard_map/ppermute | solution.py:127
  136.0 8.8 %collective-permute-start.21 = (bf16[224,768]{1,0:T(8,128)(2,1)S(1)}, bf16[224,768]{1,0:T(8,128)(2,1)S(1)}, u32[]{:S(2)}, u32[]{:S(2)}) collective-permute-start(bf16[224,768]{1,0:T(8,128)(2,1)S(1)} %add_convert_fusion), channel_id=1, source_target_pairs={{0,4},{4,8},{8,12},{12,16},{16,20},{20,24},{24,28},{28,32},{32,36}... | collective-permute-start | bytes 1032200 | tf_op jit(solution)/shard_map/ppermute | solution.py:127
  139.3 5.6 %collective-permute-start.13 = (bf16[224,768]{1,0:T(8,128)(2,1)S(1)}, bf16[224,768]{1,0:T(8,128)(2,1)S(1)}, u32[]{:S(2)}, u32[]{:S(2)}) collective-permute-start(bf16[224,768]{1,0:T(8,128)(2,1)S(1)} %add_convert_fusion.4), channel_id=1, source_target_pairs={{0,4},{4,8},{8,12},{12,16},{16,20},{20,24},{24,28},{28,32},{32,36}... | collective-permute-start | bytes 1032200 | tf_op jit(solution)/shard_map/ppermute | solution.py:127
  145.0 15.2 %collective-permute-start.22 = (bf16[448,384]{1,0:T(8,128)(2,1)S(1)}, bf16[448,384]{1,0:T(8,128)(2,1)S(1)}, u32[]{:S(2)}, u32[]{:S(2)}) collective-permute-start(bf16[448,384]{1,0:T(8,128)(2,1)S(1)} %fusion.31), channel_id=1, source_target_pairs={{0,1},{1,0},{2,3},{3,2},{4,5},{5,4},{6,7},{7,6},{8,9},{9,8},{10,11... | collective-permute-start | bytes 1032200 | tf_op jit(solution)/shard_map/ppermute | solution.py:131
  157.0 11.7 %collective-permute-start = (bf16[72,448]{0,1:T(8,128)(2,1)S(1)}, bf16[72,448]{0,1:T(8,128)(2,1)S(1)}, u32[]{:S(2)}, u32[]{:S(2)}) collective-permute-start(bf16[72,448]{0,1:T(8,128)(2,1)S(1)} %select_bitcast_fusion), channel_id=1, source_target_pairs={{0,128},{128,0},{256,384},{384,256},{1,129},{129,1},{257,385},{385... | collective-permute-start | bytes 193544 | tf_op jit(solution)/shard_map/ppermute | solution.py:140
  161.3 20.2 %all-to-all-start.2 = ((f32[32,8,128]{2,1,0:T(8,128)}), f32[32,8,128]{2,1,0:T(8,128)S(1)}, u32[]{:S(2)}, u32[]{:S(2)}) async-start(f32[32,8,128]{2,1,0:T(8,128)} %broadcast_in_dim.74), calls=%async_computation.2 | async-start | bytes 262144 | tf_op jit(solution)/shard_map/all_to_all | solution.py:21
  168.9 7.9 %collective-permute-start.1 = (bf16[72,448]{0,1:T(8,128)(2,1)S(1)}, bf16[72,448]{0,1:T(8,128)(2,1)S(1)}, u32[]{:S(2)}, u32[]{:S(2)}) collective-permute-start(bf16[72,448]{0,1:T(8,128)(2,1)S(1)} %fusion.55), channel_id=1, source_target_pairs={{0,256},{128,384},{256,0},{384,128},{1,257},{129,385},{257,1},{385... | collective-permute-start | bytes 193544 | tf_op jit(solution)/shard_map/ppermute | solution.py:140
  176.8 13.6 %collective-permute-start.2 = (bf16[72,448]{0,1:T(8,128)(2,1)S(1)}, bf16[72,448]{0,1:T(8,128)(2,1)S(1)}, u32[]{:S(2)}, u32[]{:S(2)}) collective-permute-start(bf16[72,448]{0,1:T(8,128)(2,1)S(1)} %add.122), channel_id=1, source_target_pairs={{0,64},{64,0},{1,65},{65,1},{2,66},{66,2},{3,67},{67,3},{4,68},{68... | collective-permute-start | bytes 193544 | tf_op jit(solution)/shard_map/ppermute | solution.py:140
  182.1 19.9 %all-to-all-start.3 = ((f32[16,8,128]{2,1,0:T(8,128)}), f32[16,8,128]{2,1,0:T(8,128)S(1)}, u32[]{:S(2)}, u32[]{:S(2)}) async-start(f32[16,8,128]{2,1,0:T(8,128)} %broadcast_in_dim.75), calls=%async_computation.3 | async-start | bytes 131072 | tf_op jit(solution)/shard_map/all_to_all | solution.py:21
